TPU v7x, 256 devices: a whole 4x4x8 slice. The times are simulated.
256 devices in a mesh: ctx: 32 (over z_hi, y, core), tp: 8 (over z_lo, x).
Axes of the slice: x: 4, y: 4, z: 8 (z_hi: 4, z_lo: 2; z = z_hi * 2 + z_lo), core: 2. Of those that a mesh axis runs over, the one named last changes fastest.
Arguments:
- queries: bfloat16 [4096, 8192], P('ctx', 'tp'), may hold values from -256 to 256
- keys: bfloat16 [4096, 1024], P(('ctx', 'tp')), may hold values from -6.5 to 6.5
- values: bfloat16 [4096, 1024], P(('ctx', 'tp')), may hold values from -6 to 6
- output_gradient: bfloat16 [4096, 8192], P('ctx', 'tp'), may hold values from -6 to 6
- span_order: int32 [64], replicated, may hold values from 0 to 63, as said below
Outputs:
- query_grad: bfloat16 [4096, 8192], P('ctx', 'tp')
- key_gradient_rows: bfloat16 [4096, 1024], P(('ctx', 'tp'))
- value_gradient_rows: bfloat16 [4096, 1024], P(('ctx', 'tp'))
Inputs may be any that keep to these rules, and one draw needn't show every extreme that they name: `span_order`: each value 0 to 63 appears once; entries 2d and 2d + 1 sum to 63.
All inputs are finite; a program needn't handle non-finite values.
Results may differ from a plain program's by a relative error of at most 0.0073.
Values may be sent and summed in bfloat16 or wider, within the bound.
A program may use at most 64 MiB of HBM per device.

v0:
```python
import math

import jax
import jax.numpy as jnp
from jax import lax
from jax.sharding import PartitionSpec as P

HEAD_SIZE = 128
QUERY_HEADS = 64
KEY_VALUE_HEADS = 8


def in_one_piece(arrays, axis, dim, along):
    ends, at = ([], 0)
    for a in arrays[:-1]:
        at += a.shape[along]
        ends.append(at)
    both = jnp.concatenate(arrays, axis=along)
    return tuple(jnp.split(lax.all_gather(both, axis, axis=dim, tiled=True), ends, axis=along))


def split_up(shard, dim, devices):
    before, after = (shard.shape[:dim], shard.shape[dim + 1 :])
    return jnp.moveaxis(shard.reshape(*before, devices, -1, *after), dim, 0)


def sent_and_summed(shard, axis, dim):
    devices = lax.axis_size(axis)
    blocks = lax.all_to_all(split_up(shard, dim, devices), axis, 0, 0, tiled=True)
    return jnp.sum(blocks.astype(jnp.float32), axis=0)


def body(queries, keys, values, output_gradient, span_order):
    scale = HEAD_SIZE ** (-0.5)
    head_group = QUERY_HEADS // KEY_VALUE_HEADS
    k_local, v_local = (
        lax.all_to_all(keys, "tp", split_axis=1, concat_axis=0, tiled=True),
        lax.all_to_all(values, "tp", split_axis=1, concat_axis=0, tiled=True),
    )
    tokens_here = queries.shape[0]
    kv_heads = k_local.shape[1] // HEAD_SIZE
    whole_k, whole_v = in_one_piece((k_local, v_local), "ctx", 0, 1)
    length = whole_k.shape[0]
    span = tokens_here // 2
    ctx_index = lax.axis_index("ctx")
    own_spans = lax.dynamic_slice_in_dim(span_order, 2 * ctx_index, 2)
    local_rows = jnp.arange(tokens_here, dtype=jnp.int32)
    own_pos = (
        jnp.repeat(own_spans, span, total_repeat_length=tokens_here) * span + local_rows % span
    )
    query_pos = jnp.tile(own_pos, head_group)
    all_rows = jnp.arange(length, dtype=jnp.int32)
    all_pos = jnp.repeat(span_order, span, total_repeat_length=length) * span + all_rows % span
    q_rows = (
        queries.reshape(tokens_here, kv_heads, head_group, HEAD_SIZE)
        .transpose(1, 2, 0, 3)
        .reshape(kv_heads, head_group * tokens_here, HEAD_SIZE)
    )
    g_rows = (
        output_gradient.reshape(tokens_here, kv_heads, head_group, HEAD_SIZE)
        .transpose(1, 2, 0, 3)
        .reshape(kv_heads, head_group * tokens_here, HEAD_SIZE)
    )

    def scores(k_block, pos_block):
        score = (
            jnp.einsum("gqd,gkd->gqk", q_rows, k_block, preferred_element_type=jnp.float32) * scale
        )
        return (score, query_pos[:, None] >= pos_block[None, :])

    width = math.gcd(whole_k.shape[0], 256)
    count = whole_k.shape[0] // width
    k_blocks = whole_k.reshape(count, width, kv_heads, HEAD_SIZE).transpose(0, 2, 1, 3)
    v_blocks = whole_v.reshape(count, width, kv_heads, HEAD_SIZE).transpose(0, 2, 1, 3)
    k_blocks, v_blocks, pos_blocks = (k_blocks, v_blocks, all_pos.reshape(count, width))

    def stats_step(carry, items):
        top, total = carry
        k_block, pos_block = items
        score, visible = scores(k_block, pos_block)
        score = jnp.where(visible[None], score, -1e30)
        new_top = jnp.maximum(top, jnp.max(score, axis=-1))
        expo = jnp.where(visible[None], jnp.exp(score - new_top[..., None]), 0.0)
        total = total * jnp.exp(top - new_top) + jnp.sum(expo, axis=-1)
        return ((new_top, total), None)

    start_top = jnp.full((kv_heads, head_group * tokens_here), -1e30, jnp.float32)
    start_total = jnp.zeros((kv_heads, head_group * tokens_here), jnp.float32)
    (top, total), _ = lax.scan(stats_step, (start_top, start_total), (k_blocks, pos_blocks))

    def probs(k_block, v_block, pos_block):
        score, visible = scores(k_block, pos_block)
        prob = jnp.where(visible[None], jnp.exp(score - top[..., None]), 0.0) / total[..., None]
        dprob = jnp.einsum("gqd,gkd->gqk", g_rows, v_block, preferred_element_type=jnp.float32)
        return (prob, dprob)

    def delta_step(carry, items):
        prob, dprob = probs(*items)
        return (carry + jnp.sum(prob * dprob, axis=-1), None)

    delta, _ = lax.scan(delta_step, jnp.zeros_like(total), (k_blocks, v_blocks, pos_blocks))

    def block_grads(k_block, v_block, pos_block):
        prob, dprob = probs(k_block, v_block, pos_block)
        dscore = (prob * (dprob - delta[..., None]) * scale).astype(jnp.bfloat16)
        return (prob, dscore)

    def key_value_terms(prob, dscore):
        key_gradient = jnp.einsum(
            "gqk,gqd->kgd", dscore, q_rows, preferred_element_type=jnp.float32
        )
        value_gradient = jnp.einsum(
            "gqk,gqd->kgd", prob.astype(jnp.bfloat16), g_rows, preferred_element_type=jnp.float32
        )
        return (key_gradient, value_gradient)

    start_dq = jnp.zeros((kv_heads, head_group * tokens_here, HEAD_SIZE), jnp.float32)

    def grad_step(carry, items):
        prob, dscore = block_grads(*items)
        carry = carry + jnp.einsum(
            "gqk,gkd->gqd", dscore, items[0], preferred_element_type=jnp.float32
        )
        return (carry, key_value_terms(prob, dscore))

    dquery, (dkey_terms, dvalue_terms) = lax.scan(
        grad_step, start_dq, (k_blocks, v_blocks, pos_blocks)
    )
    dkey_terms = dkey_terms.reshape(length, kv_heads * HEAD_SIZE)
    dvalue_terms = dvalue_terms.reshape(length, kv_heads * HEAD_SIZE)
    key_sum, value_sum = (
        sent_and_summed(dkey_terms.astype(jnp.bfloat16), "ctx", 0),
        sent_and_summed(dvalue_terms.astype(jnp.bfloat16), "ctx", 0),
    )
    dquery = (
        dquery.reshape(kv_heads, head_group, tokens_here, HEAD_SIZE)
        .transpose(2, 0, 1, 3)
        .reshape(tokens_here, kv_heads * head_group * HEAD_SIZE)
    )
    key_out, value_out = (
        lax.all_to_all(key_sum.astype(jnp.bfloat16), "tp", split_axis=0, concat_axis=1, tiled=True),
        lax.all_to_all(
            value_sum.astype(jnp.bfloat16), "tp", split_axis=0, concat_axis=1, tiled=True
        ),
    )
    return (dquery.astype(jnp.bfloat16), key_out, value_out)


def solution(mesh):
    return jax.shard_map(
        body,
        mesh=mesh,
        in_specs=(
            P("ctx", "tp"),
            P(("ctx", "tp"), None),
            P(("ctx", "tp"), None),
            P("ctx", "tp"),
            P(),
        ),
        out_specs=(P("ctx", "tp"), P(("ctx", "tp"), None), P(("ctx", "tp"), None)),
        check_vma=False,
    )
```

profile of v0, /device:TPU:1, one launch (start us, length us, event | category | flops | bytes accessed | tf_op | source)
XLA Modules:
  0.0 258.3 jit_solution(15043214540717424396)
XLA Ops:
  8.6 6.2 %all-to-all-start = ((bf16[16,8,128]{2,0,1:T(8,128)(2,1)}), bf16[16,8,128]{2,0,1:T(8,128)(2,1)S(1)}, u32[]{:S(2)}, u32[]{:S(2)}) async-start(bf16[16,8,128]{2,0,1:T(8,128)(2,1)} %copy_bitcast_fusion.4), calls=%async_computation | async-start | bytes 65536 | tf_op jit(solution)/shard_map/all_to_all | solution.py:37
  15.6 4.3 %all-to-all-done = bf16[16,8,128]{2,0,1:T(8,128)(2,1)S(1)} async-done(((bf16[16,8,128]{2,0,1:T(8,128)(2,1)}), bf16[16,8,128]{2,0,1:T(8,128)(2,1)S(1)}, u32[]{:S(2)}, u32[]{:S(2)}) %all-to-all-start) | async-done | bytes 32800 | tf_op jit(solution)/shard_map/all_to_all | solution.py:37
  19.9 7.5 %all_to_all.86 = bf16[16,8,128]{2,0,1:T(8,128)(2,1)S(1)} all-to-all(bf16[16,8,128]{2,0,1:T(8,128)(2,1)S(1)} %copy_bitcast_fusion.3), channel_id=1, replica_groups=mesh['ctx'=32,'tp'=8] {'tp'}, dimensions={1} | all-to-all | bytes 65536 | tf_op jit(solution)/shard_map/all_to_all | solution.py:38
  28.8 1.6 fusion.67
  30.4 2.1 fusion.64
  32.5 2.1 fusion.65
  34.5 2.1 fusion.66
  37.4 4.5 %compare_select_fusion.2 = (s32[4096,1]{0,1:T(1,128)S(1)}, s32[4096,1]{0,1:T(1,128)S(1)}) fusion(s32[]{:T(128)} %bitcast.59, s32[]{:T(128)} %bitcast.60, s32[]{:T(128)} %bitcast.61, s32[]{:T(128)} %bitcast.62, s32[]{:T(128)} %bitcast.63, s32[]{:T(128)} %bitcast.65, s32[]{:T(128)} %bitcast.64, s32[4096,1]{0,1:T(1,128)S(1)} %bitcast.341, ...), kind=kLoop, calls=%fused_computation.133 | loop fusion | flops 57344 | bytes 65564 | tf_op jit(solution)/shard_map/jit(_take)/gather | solution.py:53
  41.9 2.9 %compare_reduce_fusion.56 = (pred[4096]{0:T(1024)(128)(4,1)S(1)}, pred[4096]{0:T(1024)(128)(4,1)S(1)}, pred[4096]{0:T(1024)(128)(4,1)S(1)}, pred[4096]{0:T(1024)...) fusion(s32[4096,1]{0,1:T(1,128)S(1)} %get-tuple-element.418), kind=kLoop, calls=%fused_computation.132 | loop fusion | flops 233472 | bytes 249856 | tf_op jit(solution)/shard_map/jit(_take)/gather | solution.py:53
  44.8 35.9 %select_multiply_fusion = s32[4096]{0:T(1024)S(1)} fusion(pred[4096]{0:T(1024)(128)(4,1)S(1)} %get-tuple-element.356, pred[4096]{0:T(1024)(128)(4,1)S(1)} %get-tuple-element.355, pred[4096]{0:T(1024)(128)(4,1)S(1)} %get-tuple-element.354, pred[4096]{0:T(1024)(128)(4,1)S(1)} %get-tuple-element.353, pred[4096]{0:T(1024)(128)(4,1)S(1)} %get-tuple-element.352, ...), kind=kLoop, calls=%fused_computation.150 | loop fusion | flops 237568 | bytes 266468 | tf_op jit(solution)/shard_map/mul | solution.py:53
  80.7 1.0 copy.41
  82.5 1.3 fusion.60
  83.8 2.3 all-gather.2.cloned.1.call-done
  86.1 1.7 fusion.62
  87.8 10.6 %while.41 = (s32[]{:T(128)}, f32[1,1024]{1,0:T(1,128)S(1)}, f32[1,1024]{1,0:T(1,128)S(1)}, s32[16,256]{1,0:T(8,128)S(1)}, bf16[16,1,256,128]{3,2,1,0:T(8,128)(2,...) while((s32[]{:T(128)}, f32[1,1024]{1,0:T(1,128)S(1)}, ...), condition=%wide.region_3.4_spmd.clone, body=%wide.region_0.3_spmd.clone.sunk | while | flops 69211136 | bytes 2495096 | solution.py:89
  98.5 12.7 %while.42 = (s32[]{:T(128)}, f32[1,1024]{1,0:T(1,128)S(1)}, s32[16,256]{1,0:T(8,128)S(1)}, bf16[16,1,256,128]{3,2,1,0:T(8,128)(2,1)S(1)}, bf16[1,1024,128]{2,1,0...) while((s32[]{:T(128)}, f32[1,1024]{1,0:T(1,128)S(1)}, ...), condition=%wide.region_6.7_spmd.clone, body=%wide.region_4.6_spmd.clone.sunk | while | flops 136053760 | bytes 2789011 | solution.py:101
  111.2 48.2 %while.43 = (s32[]{:T(128)}, f32[1,1024,128]{2,1,0:T(8,128)S(1)}, bf16[16,256,1,128]{3,1,2,0:T(8,128)(2,1)}, bf16[16,256,1,128]{3,1,2,0:T(8,128)(2,1)}, s32[16,2...) while((s32[]{:T(128)}, f32[1,1024,128]{2,1,0:T(8,128)S(1)}, ...), condition=%wide.region_8.9_spmd.clone, body=%wide.region_7.8_spmd.clone.sunk | while | flops 338427904 | bytes 7298743 | solution.py:126
  112.0 0.9 fusion.125
  113.3 0.9 fusion.124
  115.0 0.9 fusion.125
  118.0 0.9 fusion.125
  119.4 0.9 fusion.124
  122.4 0.9 fusion.124
  124.0 0.9 fusion.125
  125.4 0.9 fusion.124
  127.0 0.9 fusion.125
  128.4 0.9 fusion.124
  130.0 0.9 fusion.125
  131.4 0.9 fusion.124
  133.1 0.9 fusion.125
  134.4 0.9 fusion.124
  140.4 0.9 fusion.124
  142.1 0.9 fusion.125
  145.1 0.9 fusion.125
  146.4 0.9 fusion.124
  151.1 0.9 fusion.125
  152.5 0.9 fusion.124
  154.1 0.9 fusion.125
  155.5 0.9 fusion.124
  157.1 0.9 fusion.125
  158.5 0.9 fusion.124
  159.4 40.1 %all_to_all.87 = bf16[32,128,128]{2,1,0:T(8,128)(2,1)S(1)} all-to-all(bf16[32,128,128]{2,1,0:T(8,128)(2,1)} %bitcast.319), channel_id=1, replica_groups=mesh['ctx'=32,'tp'=8] {'ctx'}, dimensions={0} | all-to-all | bytes 2097152 | tf_op jit(solution)/shard_map/all_to_all | solution.py:29
  199.5 5.6 %all-to-all-start.2 = ((bf16[32,128,128]{2,1,0:T(8,128)(2,1)}), bf16[32,128,128]{2,1,0:T(8,128)(2,1)S(1)}, u32[]{:S(2)}, u32[]{:S(2)}) async-start(bf16[32,128,128]{2,1,0:T(8,128)(2,1)} %bitcast.320), calls=%async_computation.2 | async-start | bytes 2097152 | tf_op jit(solution)/shard_map/all_to_all | solution.py:29
  205.8 27.8 %all-to-all-done.2 = bf16[32,128,128]{2,1,0:T(8,128)(2,1)S(1)} async-done(((bf16[32,128,128]{2,1,0:T(8,128)(2,1)}), bf16[32,128,128]{2,1,0:T(8,128)(2,1)S(1)}, u32[]{:S(2)}, u32[]{:S(2)}) %all-to-all-start.2) | async-done | bytes 1048608 | tf_op jit(solution)/shard_map/all_to_all | solution.py:29
  233.7 3.3 %all-to-all-start.5 = ((bf16[8,16,128]{2,1,0:T(8,128)(2,1)}), bf16[8,16,128]{2,1,0:T(8,128)(2,1)S(1)}, u32[]{:S(2)}, u32[]{:S(2)}) async-start(bf16[8,16,128]{2,1,0:T(8,128)(2,1)} %bitcast.87), calls=%async_computation.5 | async-start | bytes 65536 | tf_op jit(solution)/shard_map/all_to_all | solution.py:142
  238.8 3.7 %all-to-all-done.5 = bf16[8,16,128]{2,1,0:T(8,128)(2,1)S(1)} async-done(((bf16[8,16,128]{2,1,0:T(8,128)(2,1)}), bf16[8,16,128]{2,1,0:T(8,128)(2,1)S(1)}, u32[]{:S(2)}, u32[]{:S(2)}) %all-to-all-start.5) | async-done | bytes 32800 | tf_op jit(solution)/shard_map/all_to_all | solution.py:142
  242.4 3.3 %all-to-all-start.3 = ((bf16[8,16,128]{2,1,0:T(8,128)(2,1)}), bf16[8,16,128]{2,1,0:T(8,128)(2,1)S(1)}, u32[]{:S(2)}, u32[]{:S(2)}) async-start(bf16[8,16,128]{2,1,0:T(8,128)(2,1)} %bitcast.84), calls=%async_computation.3 | async-start | bytes 65536 | tf_op jit(solution)/shard_map/all_to_all | solution.py:141
  246.4 4.4 %all-to-all-done.3 = bf16[8,16,128]{2,1,0:T(8,128)(2,1)S(1)} async-done(((bf16[8,16,128]{2,1,0:T(8,128)(2,1)}), bf16[8,16,128]{2,1,0:T(8,128)(2,1)S(1)}, u32[]{:S(2)}, u32[]{:S(2)}) %all-to-all-start.3) | async-done | bytes 32800 | tf_op jit(solution)/shard_map/all_to_all | solution.py:141
  (313 shorter events, 56.3 us)
Async XLA Ops:
  7.2 0.8 copy-start
  7.2 75.3 %copy-start.2 = (pred[128]{0:T(512)(128)(4,1)S(1)}, pred[128]{0:T(512)(128)(4,1)}, u32[]{:S(2)}) copy-start(pred[128]{0:T(512)(128)(4,1)} %constant.325) | copy-start | bytes 388
  7.9 73.8 %copy-start.1 = (bf16[128,1024]{1,0:T(8,128)(2,1)S(1)}, bf16[128,1024]{1,0:T(8,128)(2,1)}, u32[]{:S(2)}) copy-start(bf16[128,1024]{1,0:T(8,128)(2,1)} %param.18) | copy-start | bytes 786436
  8.6 11.3 %all-to-all-start = ((bf16[16,8,128]{2,0,1:T(8,128)(2,1)}), bf16[16,8,128]{2,0,1:T(8,128)(2,1)S(1)}, u32[]{:S(2)}, u32[]{:S(2)}) async-start(bf16[16,8,128]{2,0,1:T(8,128)(2,1)} %copy_bitcast_fusion.4), calls=%async_computation | async-start | bytes 65536 | tf_op jit(solution)/shard_map/all_to_all | solution.py:37
  14.7 71.4 %all-gather.2.cloned.1.call-start = ((), (), s32[]{:S(2)}) async-start(), calls=%async_computation.6 | async-start | bytes 2162688 | tf_op jit(solution)/shard_map/all_gather | solution.py:19
  199.5 34.2 %all-to-all-start.2 = ((bf16[32,128,128]{2,1,0:T(8,128)(2,1)}), bf16[32,128,128]{2,1,0:T(8,128)(2,1)S(1)}, u32[]{:S(2)}, u32[]{:S(2)}) async-start(bf16[32,128,128]{2,1,0:T(8,128)(2,1)} %bitcast.320), calls=%async_computation.2 | async-start | bytes 2097152 | tf_op jit(solution)/shard_map/all_to_all | solution.py:29
  233.7 8.8 %all-to-all-start.5 = ((bf16[8,16,128]{2,1,0:T(8,128)(2,1)}), bf16[8,16,128]{2,1,0:T(8,128)(2,1)S(1)}, u32[]{:S(2)}, u32[]{:S(2)}) async-start(bf16[8,16,128]{2,1,0:T(8,128)(2,1)} %bitcast.87), calls=%async_computation.5 | async-start | bytes 65536 | tf_op jit(solution)/shard_map/all_to_all | solution.py:142
  242.4 8.4 %all-to-all-start.3 = ((bf16[8,16,128]{2,1,0:T(8,128)(2,1)}), bf16[8,16,128]{2,1,0:T(8,128)(2,1)S(1)}, u32[]{:S(2)}, u32[]{:S(2)}) async-start(bf16[8,16,128]{2,1,0:T(8,128)(2,1)} %bitcast.84), calls=%async_computation.3 | async-start | bytes 65536 | tf_op jit(solution)/shard_map/all_to_all | solution.py:141
Sparse Core Ops, SparseCore 0:
  28.1 57.9 all-gather.1
where the time goes:
time: 260 us; the launch traced here: 258 us
  matrix products  64.2 us (25%)
  other arithmetic  52.2 us (20%)
  blocking collectives  47.5 us (18%)
  waiting for transfers between devices  42.5 us (16%)
  starting transfers between devices  18.5 us (7%)
  local copies, waits for them, and re-layouts  16.8 us (6%)
  between operations  14.3 us (6%)
    all_to_all x1, blocking collectives, sent_and_summed(): lax.all_to_all(split_up(shard, dim, devices), axis, 0, 0, tiled=True)  40.1 us
    mul x1, other arithmetic, body(): jnp.repeat(span_order, span, total_repeat_length=length) * span  35.9 us
    all_to_all x1, waiting for transfers between devices, sent_and_summed(): lax.all_to_all(split_up(shard, dim, devices), axis, 0, 0, tiled=True)  27.8 us
    dot_general x48, matrix products, scores(): jnp.einsum('gqd,gkd->gqk', q_rows, k_block, preferred_element_type=jnp.fl...  18.1 us
    dot_general x16, matrix products, key_value_terms(): jnp.einsum('gqk,gqd->kgd', dscore, q_rows, preferred_element_type=jnp.flo...  14.6 us
    dot_general x16, matrix products, key_value_terms(): jnp.einsum('gqk,gqd->kgd', prob.astype(jnp.bfloat16), g_rows, preferred_e...  14.5 us
    dot_general x32, matrix products, probs(): jnp.einsum('gqd,gkd->gqk', g_rows, v_block, preferred_element_type=jnp.fl...  9.74 us
    gather x4, local copies, waits for them, and re-layouts, body(): jnp.repeat(span_order, span, total_repeat_length=length) * span  7.81 us
  transfers between devices with their start and end apart: 5, of which 5 were waited for; matrix products, arithmetic and copies ran while one was open for 23% of the time, Pallas kernels for 0%

commit v1 on v0

v1 whole, which is shorter than its diff:
```python
import functools
import math

import jax
import jax.numpy as jnp
from jax import lax
from jax.experimental import pallas as pl
from jax.experimental.pallas import tpu as pltpu
from jax.sharding import PartitionSpec as P

HEAD = 128
SPAN = 64
KV_HEADS = 8
NY = 4
NZ = 4
SCALE = HEAD**-0.5
EXPO = SCALE * math.log2(math.e)
NEG = -1e30
MESH = pl.DeviceIdType.MESH
F32 = jnp.float32
BF16 = jnp.bfloat16


def dot(a, b):
    return jnp.dot(a, b, preferred_element_type=F32)


def kernel(
    tps,
    heads,
    span,
    q_hbm,
    k_hbm,
    v_hbm,
    g_hbm,
    dq_out,
    k_out,
    v_out,
    kvst,
    kv,
    qs,
    gs,
    qn,
    gn,
    qt,
    gt,
    klo_s,
    kc_s,
    klot_s,
    kct_s,
    vlo_s,
    vc_s,
    s_s,
    d_s,
    s3_s,
    d3_s,
    st,
    st_in,
    cs,
    dqt,
    dk3,
    dqsend,
    dqrecv,
    out,
    ro,
    ry,
    rzo,
    rz,
    zs,
    fin,
    kvo,
    loc,
    a2a,
    zsem_s,
    zsem_r,
    ysem_s,
    ysem_r,
    pair_s,
    pair_r,
    yo_s,
    yo_r,
    yf_s,
    yf_r,
    zr_s,
    zr_r,
):
    rows = heads * SPAN
    toks = 2 * SPAN
    tt = toks // tps
    c = lax.axis_index("ctx")
    t = lax.axis_index("tp")
    core = lax.rem(c, 2)
    y = lax.rem(c // 2, NY)
    z = c // (2 * NY)

    def ctx_of(zz, yy, cc):
        return (zz * NY + yy) * 2 + cc

    y_up, y_dn, y_op = lax.rem(y + 1, NY), lax.rem(y + 3, NY), lax.rem(y + 2, NY)
    z_up, z_dn, z_op = lax.rem(z + 1, NZ), lax.rem(z + 3, NZ), lax.rem(z + 2, NZ)
    dev_yu, dev_yd = (ctx_of(z, y_up, core), t), (ctx_of(z, y_dn, core), t)
    dev_zu, dev_zd = (ctx_of(z_up, y, core), t), (ctx_of(z_dn, y, core), t)
    dev_pair = (ctx_of(z, y, 1 - core), t)

    def remote(src, dst, send, recv, device):
        return pltpu.make_async_remote_copy(
            src_ref=src,
            dst_ref=dst,
            send_sem=send,
            recv_sem=recv,
            device_id=device,
            device_id_type=MESH,
        )

    def landed(ref, sem):
        pltpu.make_async_copy(ref, ref, sem).wait()

    own_rows = pl.ds(pl.multiple_of(t * tt, tt), tt)
    for g in range(tps):
        cols = pl.ds(g * HEAD, HEAD)
        pltpu.make_async_copy(k_hbm.at[:, cols], kvst.at[g, 0], loc.at[0]).start()
        pltpu.make_async_copy(v_hbm.at[:, cols], kvst.at[g, 1], loc.at[0]).start()
    own_cols = pl.ds(pl.multiple_of(t * HEAD, HEAD), HEAD)
    pltpu.make_async_copy(k_hbm.at[:, own_cols], kv.at[z, y, 0, own_rows], a2a.at[1]).start()
    pltpu.make_async_copy(v_hbm.at[:, own_cols], kv.at[z, y, 1, own_rows], a2a.at[1]).start()
    for h in range(heads):
        cols = pl.ds(h * HEAD, HEAD)
        pltpu.make_async_copy(q_hbm.at[:, cols], qs.at[0, h], loc.at[1]).start()
        pltpu.make_async_copy(g_hbm.at[:, cols], gs.at[0, h], loc.at[2]).start()

    barrier = pltpu.get_barrier_semaphore()
    for o in range(1, tps):
        pl.semaphore_signal(
            barrier, inc=1, device_id=(c, lax.rem(t + o, tps)), device_id_type=MESH
        )
    for device in (dev_yu, dev_yd, dev_zu, dev_zd, dev_pair):
        pl.semaphore_signal(barrier, inc=1, device_id=device, device_id_type=MESH)
    landed(kvst, loc.at[0])
    pl.semaphore_wait(barrier, tps - 1 + 5)

    for o in range(1, tps):
        to = lax.rem(t + o, tps)
        remote(kvst.at[to], kv.at[z, y, :, own_rows], a2a.at[0], a2a.at[1], (c, to)).start()
    landed(qs.at[0], loc.at[1])
    q_copy = remote(qs.at[0], qs.at[1], pair_s.at[0], pair_r.at[0], dev_pair)
    q_copy.start()
    landed(gs.at[0], loc.at[2])
    g_copy = remote(gs.at[0], gs.at[1], pair_s.at[1], pair_r.at[1], dev_pair)
    g_copy.start()

    def spans(cc):
        s0, s1 = span[2 * cc], span[2 * cc + 1]
        return s0 > s1, jnp.minimum(s0, s1)

    devs = (c, ctx_of(z, y, 1 - core))
    flips, lows = zip(*[spans(d) for d in devs])

    def prepare(a):
        for src, normal, turned in ((qs, qn, qt), (gs, gn, gt)):
            first = src[a, :, 0:SPAN, :].reshape(rows, HEAD)
            second = src[a, :, SPAN : 2 * SPAN, :].reshape(rows, HEAD)
            lo = jnp.where(flips[a], second, first)
            hi = jnp.where(flips[a], first, second)
            normal[a, :, 0:HEAD] = lo
            normal[a, :, HEAD : 2 * HEAD] = hi
            turned[a, 0:HEAD, :] = lo.T
            turned[a, HEAD : 2 * HEAD, :] = hi.T

    def z_of(gi):
        return lax.rem(z + gi + (gi // 2) * (1 - 2 * (gi % 2)), NZ)

    def y_start(gi):
        b = kv.at[z_of(gi), y]
        remote(b, b, ysem_s.at[gi, 0], ysem_r.at[gi, 0], dev_yu).start()
        remote(b, b, ysem_s.at[gi, 1], ysem_r.at[gi, 1], dev_yd).start()

    def y_relay(gi):
        zg = z_of(gi)
        landed(kv.at[zg, y_dn], ysem_r.at[gi, 0])
        b = kv.at[zg, y_dn, 0]
        remote(b, b, ysem_s.at[gi, 2], ysem_r.at[gi, 2], dev_yu).start()
        landed(kv.at[zg, y_up], ysem_r.at[gi, 1])
        b = kv.at[zg, y_up, 1]
        remote(b, b, ysem_s.at[gi, 3], ysem_r.at[gi, 3], dev_yd).start()

    def y_finish(gi):
        zg = z_of(gi)
        landed(kv.at[zg, y_op, 0], ysem_r.at[gi, 2])
        landed(kv.at[zg, y_op, 1], ysem_r.at[gi, 3])

    own = kv.at[z, y]
    landed(own, a2a.at[1])
    remote(own, own, zsem_s.at[0], zsem_r.at[0], dev_zu).start()
    remote(own, own, zsem_s.at[1], zsem_r.at[1], dev_zd).start()
    y_start(0)

    prepare(0)

    def lohi(zg, yy, w):
        first, second = kv[zg, yy, w, 0:SPAN, :], kv[zg, yy, w, SPAN : 2 * SPAN, :]
        flip, _ = spans(ctx_of(zg, yy, core))
        return jnp.where(flip, second, first), jnp.where(flip, first, second)

    key_i = lax.broadcasted_iota(jnp.int32, (SPAN, rows), 0)
    tok_i = lax.rem(lax.broadcasted_iota(jnp.int32, (SPAN, rows), 1), SPAN)
    hidden = key_i > tok_i

    kself, vself = lohi(z, y, 0)[0], lohi(z, y, 1)[0]
    s3 = jnp.where(hidden, NEG, dot(kself, qt[0, 0:HEAD, :]))
    d3 = dot(vself, gt[0, 0:HEAD, :])
    s3_s[...] = s3
    d3_s[...] = d3
    m3 = jnp.max(s3, axis=0, keepdims=True)
    e3 = jnp.exp2((s3 - m3) * EXPO)
    none = jnp.full((1, rows), NEG, F32)
    zero = jnp.zeros((1, rows), F32)
    st[0, 0:1, :] = m3
    st[0, 1:2, :] = jnp.sum(e3, axis=0, keepdims=True)
    st[0, 2:3, :] = jnp.sum(e3 * d3, axis=0, keepdims=True)
    st[0, 3:4, :] = none
    st[0, 4:8, :] = jnp.zeros((4, rows), F32)
    st[1, 0:1, :] = none
    st[1, 1:3, :] = jnp.zeros((2, rows), F32)
    st[1, 3:4, :] = none
    st[1, 4:8, :] = jnp.zeros((4, rows), F32)

    q_copy.wait_recv()
    g_copy.wait_recv()
    prepare(1)

    landed(kv.at[z_dn, y], zsem_r.at[0])
    b = kv.at[z_dn, y, 0]
    remote(b, b, zsem_s.at[2], zsem_r.at[2], dev_zu).start()
    landed(kv.at[z_up, y], zsem_r.at[1])
    b = kv.at[z_up, y, 1]
    remote(b, b, zsem_s.at[3], zsem_r.at[3], dev_zd).start()
    y_start(1)
    y_start(2)
    y_relay(0)
    landed(kv.at[z_op, y, 0], zsem_r.at[2])
    landed(kv.at[z_op, y, 1], zsem_r.at[3])
    y_start(3)

    def picks(zg, a):
        return [spans(ctx_of(zg, yy, core))[1] < lows[a] for yy in range(NY)]

    def block(yy):
        return slice(yy * SPAN, (yy + 1) * SPAN)

    def scores(gi):
        zg = z_of(gi)
        k = [lohi(zg, yy, 0) for yy in range(NY)]
        v = [lohi(zg, yy, 1) for yy in range(NY)]
        for yy in range(NY):
            klo_s[gi, block(yy), :] = k[yy][0]
            vlo_s[gi, block(yy), :] = v[yy][0]
        klo, vlo = klo_s[gi], vlo_s[gi]
        klot_s[gi] = klo.T
        for a in range(2):
            pick = picks(zg, a)
            for yy in range(NY):
                for half, (src, dst) in ((0, (k, kc_s)), (1, (v, vc_s))):
                    lo, hi = src[yy]
                    none_ = jnp.zeros_like(lo)
                    dst[gi, a, block(yy), 0:HEAD] = jnp.where(pick[yy], lo, none_)
                    dst[gi, a, block(yy), HEAD : 2 * HEAD] = jnp.where(pick[yy], none_, hi)
            kc, vc = kc_s[gi, a], vc_s[gi, a]
            kct_s[gi, a] = kc.T
            s1 = dot(klo, qt[a, HEAD : 2 * HEAD, :])
            d1 = dot(vlo, gt[a, HEAD : 2 * HEAD, :])
            s2 = dot(kc, qt[a])
            d2 = dot(vc, gt[a])
            s_s[gi, a, 0] = s1
            d_s[gi, a, 0] = d1
            d_s[gi, a, 1] = d2
            parts = []
            for yy in range(NY):
                part = s2[block(yy), :]
                if a == 0:
                    here = jnp.logical_and(zg == z, yy == y)
                    part = jnp.where(jnp.logical_and(hidden, here), NEG, part)
                s_s[gi, a, 1, block(yy), :] = part
                parts.append(part)
            m_lo, l_lo, e_lo = st[a, 0:1, :], st[a, 1:2, :], st[a, 2:3, :]
            m_hi, l_hi, e_hi = st[a, 3:4, :], st[a, 4:5, :], st[a, 5:6, :]
            n_lo, n_hi = m_lo, jnp.maximum(m_hi, jnp.max(s1, axis=0, keepdims=True))
            for yy in range(NY):
                top = jnp.max(parts[yy], axis=0, keepdims=True)
                n_lo = jnp.maximum(n_lo, jnp.where(pick[yy], top, none))
                n_hi = jnp.maximum(n_hi, jnp.where(pick[yy], none, top))
            f_lo, f_hi = jnp.exp2((m_lo - n_lo) * EXPO), jnp.exp2((m_hi - n_hi) * EXPO)
            l_lo, e_lo, l_hi, e_hi = l_lo * f_lo, e_lo * f_lo, l_hi * f_hi, e_hi * f_hi
            e1 = jnp.exp2((s1 - n_hi) * EXPO)
            l_hi = l_hi + jnp.sum(e1, axis=0, keepdims=True)
            e_hi = e_hi + jnp.sum(e1 * d1, axis=0, keepdims=True)
            for yy in range(NY):
                e2 = jnp.exp2((parts[yy] - jnp.where(pick[yy], n_lo, n_hi)) * EXPO)
                total = jnp.sum(e2, axis=0, keepdims=True)
                inner = jnp.sum(e2 * d2[block(yy), :], axis=0, keepdims=True)
                l_lo = l_lo + jnp.where(pick[yy], total, zero)
                l_hi = l_hi + jnp.where(pick[yy], zero, total)
                e_lo = e_lo + jnp.where(pick[yy], inner, zero)
                e_hi = e_hi + jnp.where(pick[yy], zero, inner)
            st[a, 0:1, :] = n_lo
            st[a, 1:2, :] = l_lo
            st[a, 2:3, :] = e_lo
            st[a, 3:4, :] = n_hi
            st[a, 4:5, :] = l_hi
            st[a, 5:6, :] = e_hi

    def score_step(gi, carry):
        @pl.when(gi < NZ - 1)
        def _():
            y_relay(gi + 1)

        y_finish(gi)
        scores(gi)
        return carry

    lax.fori_loop(0, NZ, score_step, 0)

    st_copy = remote(st, st_in, pair_s.at[2], pair_r.at[2], dev_pair)
    st_copy.start()
    dqt[...] = jnp.zeros_like(dqt)
    st_copy.wait_recv()
    for a in range(2):
        for at in (0, 3):
            m0, l0, e0 = (st[a, at + i : at + i + 1, :] for i in range(3))
            m1, l1, e1 = (st_in[1 - a, at + i : at + i + 1, :] for i in range(3))
            m = jnp.maximum(m0, m1)
            f0, f1 = jnp.exp2((m0 - m) * EXPO), jnp.exp2((m1 - m) * EXPO)
            inv = 1.0 / (l0 * f0 + l1 * f1)
            cs[a, at : at + 1, :] = m
            cs[a, at + 1 : at + 2, :] = inv
            cs[a, at + 2 : at + 3, :] = (e0 * f0 + e1 * f1) * inv

    def weights(s, d, m, inv, delta):
        prob = jnp.exp2((s - m) * EXPO) * inv
        return prob.astype(BF16), (prob * (d - delta) * SCALE).astype(BF16)

    lo_stats = [[cs[a, i : i + 1, :] for i in range(3)] for a in range(2)]
    w3, ds3 = weights(s3_s[...], d3_s[...], *lo_stats[0])
    dk3[0] = dot(ds3, qn[0, :, 0:HEAD])
    dk3[1] = dot(w3, gn[0, :, 0:HEAD])
    dqt[0, 0:HEAD, :] = dot(lohi(z, y, 0)[0].T, ds3)

    def grads(gi):
        zg = z_of(gi)
        dlo, dhi = [[None] * NY, [None] * NY], [[None] * NY, [None] * NY]
        for a in range(2):
            pick = picks(zg, a)
            lo = [cs[a, i : i + 1, :] for i in range(3)]
            hi = [cs[a, 3 + i : 4 + i, :] for i in range(3)]
            w1, ds1 = weights(s_s[gi, a, 0], d_s[gi, a, 0], *hi)
            pairs = [
                weights(
                    s_s[gi, a, 1, block(yy), :],
                    d_s[gi, a, 1, block(yy), :],
                    *[jnp.where(pick[yy], l, h) for l, h in zip(lo, hi)],
                )
                for yy in range(NY)
            ]
            w2 = jnp.concatenate([p[0] for p in pairs], axis=0)
            ds2 = jnp.concatenate([p[1] for p in pairs], axis=0)
            for i, (x1, x2, wide) in enumerate(((ds1, ds2, qn), (w1, w2, gn))):
                one = dot(x1, wide[a, :, HEAD : 2 * HEAD])
                two = dot(x2, wide[a])
                for yy in range(NY):
                    left, right = two[block(yy), 0:HEAD], two[block(yy), HEAD : 2 * HEAD]
                    none_ = jnp.zeros_like(left)
                    new_lo = one[block(yy), :] + jnp.where(pick[yy], left, none_)
                    new_hi = jnp.where(pick[yy], none_, right)
                    if a == 0:
                        here = jnp.logical_and(zg == z, yy == y)
                        new_lo = new_lo + jnp.where(here, dk3[i], none_)
                        dlo[i][yy], dhi[i][yy] = new_lo, new_hi
                    else:
                        dlo[i][yy] = dlo[i][yy] + new_lo
                        dhi[i][yy] = dhi[i][yy] + new_hi
            dqt[a] += dot(kct_s[gi, a], ds2)
            dqt[a, HEAD : 2 * HEAD, :] += dot(klot_s[gi], ds1)
        for yy in range(NY):
            flip, _ = spans(ctx_of(zg, yy, core))
            for i in range(2):
                out[zg, yy, i, 0:SPAN, :] = jnp.where(flip, dhi[i][yy], dlo[i][yy]).astype(BF16)
                out[zg, yy, i, SPAN : 2 * SPAN, :] = jnp.where(
                    flip, dlo[i][yy], dhi[i][yy]
                ).astype(BF16)

    def plus(a, b):
        return (a.astype(F32) + b.astype(F32)).astype(BF16)

    def ry_opposite(gi):
        zg = z_of(gi)
        remote(out.at[zg, y_op, 0], ro.at[gi, 0], yo_s.at[gi, 0], yo_r.at[gi, 0], dev_yu).start()
        remote(out.at[zg, y_op, 1], ro.at[gi, 1], yo_s.at[gi, 1], yo_r.at[gi, 1], dev_yd).start()

    def ry_forward(gi):
        zg = z_of(gi)
        landed(ro.at[gi, 0], yo_r.at[gi, 0])
        out[zg, y_up, 0] = plus(out[zg, y_up, 0], ro[gi, 0])
        remote(out.at[zg, y_up], ry.at[gi, 0], yf_s.at[gi, 0], yf_r.at[gi, 0], dev_yu).start()
        landed(ro.at[gi, 1], yo_r.at[gi, 1])
        out[zg, y_dn, 1] = plus(out[zg, y_dn, 1], ro[gi, 1])
        remote(out.at[zg, y_dn], ry.at[gi, 1], yf_s.at[gi, 1], yf_r.at[gi, 1], dev_yd).start()

    def ry_total(gi):
        zg = z_of(gi)
        landed(ry.at[gi, 0], yf_r.at[gi, 0])
        landed(ry.at[gi, 1], yf_r.at[gi, 1])
        return out[zg, y].astype(F32) + ry[gi, 0].astype(F32) + ry[gi, 1].astype(F32)

    def z_opposite():
        zs[2] = ry_total(3).astype(BF16)
        remote(zs.at[2, 0], rzo.at[0], zr_s.at[0], zr_r.at[0], dev_zu).start()
        remote(zs.at[2, 1], rzo.at[1], zr_s.at[1], zr_r.at[1], dev_zd).start()

    def z_down():
        total = ry_total(2)
        landed(rzo.at[1], zr_r.at[1])
        zs[1, 0] = total[0].astype(BF16)
        zs[1, 1] = (total[1] + rzo[1].astype(F32)).astype(BF16)
        remote(zs.at[1], rz.at[1], zr_s.at[3], zr_r.at[3], dev_zd).start()

    def z_up_():
        total = ry_total(1)
        landed(rzo.at[0], zr_r.at[0])
        zs[0, 0] = (total[0] + rzo[0].astype(F32)).astype(BF16)
        zs[0, 1] = total[1].astype(BF16)
        remote(zs.at[0], rz.at[0], zr_s.at[2], zr_r.at[2], dev_zu).start()

    def grad_step(i, carry):
        gi = NZ - 1 - i
        grads(gi)
        ry_opposite(gi)

        @pl.when(i >= 1)
        def _():
            ry_forward(gi + 1)

        @pl.when(i == 2)
        def _():
            z_opposite()

        @pl.when(i == 3)
        def _():
            z_down()

        return carry

    lax.fori_loop(0, NZ, grad_step, 0)

    dqsend[...] = dqt[1].astype(BF16)
    ry_forward(0)
    dq_copy = remote(dqsend, dqrecv, pair_s.at[3], pair_r.at[3], dev_pair)
    dq_copy.start()
    z_up_()
    dq_copy.wait_recv()
    total_q = dqt[0] + dqrecv[...].astype(F32)
    lo, hi = total_q[0:HEAD, :].T.astype(BF16), total_q[HEAD : 2 * HEAD, :].T.astype(BF16)
    first, second = jnp.where(flips[0], hi, lo), jnp.where(flips[0], lo, hi)
    for h in range(heads):
        dq_out[0:SPAN, h * HEAD : (h + 1) * HEAD] = first[h * SPAN : (h + 1) * SPAN, :]
        dq_out[SPAN : 2 * SPAN, h * HEAD : (h + 1) * HEAD] = second[h * SPAN : (h + 1) * SPAN, :]

    total = ry_total(0)
    landed(rz.at[0], zr_r.at[2])
    landed(rz.at[1], zr_r.at[3])
    fin[...] = (total + rz[0].astype(F32) + rz[1].astype(F32)).astype(BF16)
    for o in range(1, tps):
        to = lax.rem(t + o, tps)
        to_rows = pl.ds(pl.multiple_of(to * tt, tt), tt)
        remote(fin.at[:, to_rows], kvo.at[t], a2a.at[2], a2a.at[3], (c, to)).start()
    kvo[t] = fin[:, own_rows]

    landed(kvst.at[pl.ds(0, tps - 1)], a2a.at[0])
    q_copy.wait_send()
    g_copy.wait_send()
    st_copy.wait_send()
    dq_copy.wait_send()
    half, whole = kv.at[0, 0, 0], kv.at[0, 0]
    for i in range(4):
        landed(whole if i < 2 else half, zsem_s.at[i])
        landed(half if i < 2 else whole, zr_s.at[i])
        for gi in range(NZ):
            landed(whole if i < 2 else half, ysem_s.at[gi, i])
    for gi in range(NZ):
        for i in range(2):
            landed(half, yo_s.at[gi, i])
            landed(whole, yf_s.at[gi, i])
    landed(kvo.at[pl.ds(0, tps - 1)], a2a.at[3])
    for g in range(tps):
        k_out[:, g * HEAD : (g + 1) * HEAD] = kvo[g, 0]
        v_out[:, g * HEAD : (g + 1) * HEAD] = kvo[g, 1]
    landed(kvo.at[pl.ds(0, tps - 1)], a2a.at[2])


def body(queries, keys, values, output_gradient, span_order):
    tps = lax.axis_size("tp")
    toks, width = queries.shape
    heads = width // HEAD
    rows = heads * SPAN
    tt = keys.shape[0]
    vmem = pltpu.VMEM
    half = (toks, HEAD)
    block = (2, *half)
    group = NY * SPAN
    dma = pltpu.SemaphoreType.DMA
    scratch = [
        vmem((tps, 2, tt, HEAD), BF16),
        vmem((NZ, NY, *block), BF16),
        vmem((2, heads, *half), BF16),
        vmem((2, heads, *half), BF16),
        vmem((2, rows, 2 * HEAD), BF16),
        vmem((2, rows, 2 * HEAD), BF16),
        vmem((2, 2 * HEAD, rows), BF16),
        vmem((2, 2 * HEAD, rows), BF16),
        vmem((NZ, group, HEAD), BF16),
        vmem((NZ, 2, group, 2 * HEAD), BF16),
        vmem((NZ, HEAD, group), BF16),
        vmem((NZ, 2, 2 * HEAD, group), BF16),
        vmem((NZ, group, HEAD), BF16),
        vmem((NZ, 2, group, 2 * HEAD), BF16),
        vmem((NZ, 2, 2, group, rows), F32),
        vmem((NZ, 2, 2, group, rows), F32),
        vmem((SPAN, rows), F32),
        vmem((SPAN, rows), F32),
        vmem((2, 8, rows), F32),
        vmem((2, 8, rows), F32),
        vmem((2, 8, rows), F32),
        vmem((2, 2 * HEAD, rows), F32),
        vmem((2, SPAN, HEAD), F32),
        vmem((2 * HEAD, rows), BF16),
        vmem((2 * HEAD, rows), BF16),
        vmem((NZ, NY, *block), BF16),
        vmem((NZ, *block), BF16),
        vmem((NZ, 2, *block), BF16),
        vmem(block, BF16),
        vmem((2, *block), BF16),
        vmem((3, *block), BF16),
        vmem(block, BF16),
        vmem((tps, 2, tt, HEAD), BF16),
        dma((3,)),
        dma((4,)),
        dma((4,)),
        dma((4,)),
        dma((NZ, 4)),
        dma((NZ, 4)),
        dma((4,)),
        dma((4,)),
        dma((NZ, 2)),
        dma((NZ, 2)),
        dma((NZ, 2)),
        dma((NZ, 2)),
        dma((4,)),
        dma((4,)),
    ]
    anywhere = pl.BlockSpec(memory_space=pl.ANY)
    in_vmem = pl.BlockSpec(memory_space=pltpu.VMEM)
    return tuple(
        pl.pallas_call(
            functools.partial(kernel, tps, heads),
            out_shape=(
                jax.ShapeDtypeStruct(queries.shape, BF16),
                jax.ShapeDtypeStruct(keys.shape, BF16),
                jax.ShapeDtypeStruct(values.shape, BF16),
            ),
            in_specs=[pl.BlockSpec(memory_space=pltpu.SMEM)] + [anywhere] * 4,
            out_specs=(in_vmem,) * 3,
            scratch_shapes=scratch,
            compiler_params=pltpu.CompilerParams(
                collective_id=0, has_side_effects=True, vmem_limit_bytes=56 * 1024 * 1024
            ),
        )(span_order, queries, keys, values, output_gradient)
    )


def solution(mesh):
    return jax.shard_map(
        body,
        mesh=mesh,
        in_specs=(
            P("ctx", "tp"),
            P(("ctx", "tp"), None),
            P(("ctx", "tp"), None),
            P("ctx", "tp"),
            P(),
        ),
        out_specs=(P("ctx", "tp"), P(("ctx", "tp"), None), P(("ctx", "tp"), None)),
        check_vma=False,
    )
```

time: 260 us -> 62 us (0.24)
  the two profiles are of different devices: /device:TPU:1 before, /device:TPU:32 now
where the time goes in v1:
time: 62 us; the launch traced here: 61.7 us
  Pallas kernels  58 us (94%)
  local copies, waits for them, and re-layouts  3.06 us (5%)
  between operations  0.65 us (1%)
    pallas_call x1, Pallas kernels, body(): pl.pallas_call(functools.partial(kernel, tps, heads), out_shape=(jax.Shap...  58 us
    unnamed x7, local copies, waits for them, and re-layouts  3.06 us

profile of v1, /device:TPU:32, one launch (start us, length us, event | category | flops | bytes accessed | tf_op | source)
XLA Modules:
  0.0 61.7 jit_solution(5028431417465666170)
XLA Ops:
  0.6 58.0 %shard_map.76 = (bf16[128,1024]{1,0:T(8,128)(2,1)}, bf16[16,1024]{1,0:T(8,128)(2,1)}, bf16[16,1024]{1,0:T(8,128)(2,1)}) custom-call(s32[64]{0:T(128)} %span.1, bf16[128,1024]{1,0:T(8,128)(2,1)} %q_hbm.1, bf16[16,1024]{1,0:T(8,128)(2,1)} %k_hbm.1, bf16[16,1024]{1,0:T(8,128)(2,1)} %v_hbm.1, bf16[128,1024]{1,0:T(8,128)(2,1)} %g_hbm.1), custom_call_target="tpu_custom_call" | custom-call | tf_op jit(solution)/shard_map/pallas_call | solution.py:561
  58.6 0.0 copy-start.1
  58.6 1.7 %copy.11 = bf16[128,1024]{1,0:T(8,128)(2,1)} copy(bf16[128,1024]{1,0:T(8,128)(2,1)} %get-tuple-element.6) | data formatting | bytes 524288
  60.3 0.0 copy-done.1
  60.3 0.0 copy-start
  60.3 0.6 copy.12
  60.9 0.2 copy-done
  61.1 0.6 copy.13
Async XLA Ops:
  58.6 1.7 %copy-start.1 = (bf16[16,1024]{1,0:T(8,128)(2,1)S(1)}, bf16[16,1024]{1,0:T(8,128)(2,1)}, u32[]{:S(2)}) copy-start(bf16[16,1024]{1,0:T(8,128)(2,1)} %get-tuple-element.7) | copy-start | bytes 98308
  60.3 0.8 %copy-start = (bf16[16,1024]{1,0:T(8,128)(2,1)S(1)}, bf16[16,1024]{1,0:T(8,128)(2,1)}, u32[]{:S(2)}) copy-start(bf16[16,1024]{1,0:T(8,128)(2,1)} %get-tuple-element.8) | copy-start | bytes 98308

commit v2 on v1

v2 whole, which is shorter than its diff:
```python
import functools
import math

import jax
import jax.numpy as jnp
from jax import lax
from jax.experimental import pallas as pl
from jax.experimental.pallas import tpu as pltpu
from jax.sharding import PartitionSpec as P

HEAD = 128
SPAN = 64
KV_HEADS = 8
NY = 4
NZ = 4
SCALE = HEAD**-0.5
EXPO = SCALE * math.log2(math.e)
NEG = -1e30
AG_RELAY = ()
RS_RELAY = ()
MESH = pl.DeviceIdType.MESH
F32 = jnp.float32
BF16 = jnp.bfloat16


def dot(a, b):
    return jnp.dot(a, b, preferred_element_type=F32)


def kernel(
    tps,
    heads,
    span,
    q_hbm,
    k_hbm,
    v_hbm,
    g_hbm,
    dq_out,
    k_out,
    v_out,
    kvst,
    kv,
    qs,
    gs,
    qn,
    gn,
    qt,
    gt,
    klo_s,
    kc_s,
    klot_s,
    kct_s,
    vlo_s,
    vc_s,
    s_s,
    d_s,
    s3_s,
    d3_s,
    st,
    st_in,
    cs,
    dl,
    dl_in,
    dqt,
    dk3,
    dqsend,
    dqrecv,
    out,
    ro,
    ry,
    zs,
    kvr,
    dqo,
    kvo,
    loc,
    zt_s,
    zt_r,
    ysem_s,
    ysem_r,
    pair_s,
    pair_r,
    yo_s,
    yo_r,
    yf_s,
    yf_r,
    zr_s,
    zr_r,
):
    rows = heads * SPAN
    toks = 2 * SPAN
    tt = toks // tps
    c = lax.axis_index("ctx")
    t = lax.axis_index("tp")
    core = lax.rem(c, 2)
    y = lax.rem(c // 2, NY)
    z = c // (2 * NY)

    def ctx_of(zz, yy, cc):
        return (zz * NY + yy) * 2 + cc

    y_up, y_dn, y_op = lax.rem(y + 1, NY), lax.rem(y + 3, NY), lax.rem(y + 2, NY)
    dev_yu, dev_yd = (ctx_of(z, y_up, core), t), (ctx_of(z, y_dn, core), t)
    dev_yo = (ctx_of(z, y_op, core), t)
    dev_pair = (ctx_of(z, y, 1 - core), t)

    def remote(src, dst, send, recv, device):
        return pltpu.make_async_remote_copy(
            src_ref=src,
            dst_ref=dst,
            send_sem=send,
            recv_sem=recv,
            device_id=device,
            device_id_type=MESH,
        )

    def landed(ref, sem):
        pltpu.make_async_copy(ref, ref, sem).wait()

    own_rows = pl.ds(pl.multiple_of(t * tt, tt), tt)
    own_cols = pl.ds(pl.multiple_of(t * HEAD, HEAD), HEAD)
    for w, hbm in enumerate((k_hbm, v_hbm)):
        for g in range(tps):
            pltpu.make_async_copy(
                hbm.at[:, pl.ds(g * HEAD, HEAD)], kvst.at[w, g], loc.at[w]
            ).start()
        pltpu.make_async_copy(
            hbm.at[:, own_cols], kv.at[z, y, w, own_rows], zt_r.at[w, z]
        ).start()
    for h in range(heads):
        cols = pl.ds(h * HEAD, HEAD)
        pltpu.make_async_copy(q_hbm.at[:, cols], qs.at[0, h], loc.at[2]).start()
        pltpu.make_async_copy(g_hbm.at[:, cols], gs.at[0, h], loc.at[3]).start()

    def z_of(gi):
        return lax.rem(z + gi + (gi // 2) * (1 - 2 * (gi % 2)), NZ)

    def greet(device):
        pl.semaphore_signal(barrier, inc=1, device_id=device, device_id_type=MESH)

    barrier = pltpu.get_barrier_semaphore()
    for gi in range(NZ):
        for o in range(1 if gi == 0 else 0, tps):
            greet((ctx_of(z_of(gi), y, core), lax.rem(t + o, tps)))
    for device in (dev_yu, dev_yd, dev_yo, dev_pair):
        greet(device)
    landed(kvst.at[0], loc.at[0])
    landed(kvst.at[1], loc.at[1])
    pl.semaphore_wait(barrier, NZ * tps - 1 + 4)

    for w, gi in ((0, 0), (1, 0), (0, 1), (0, 2), (0, 3), (1, 1), (1, 2), (1, 3)):
        for o in range(1 if gi == 0 else 0, tps):
            to = lax.rem(t + o, tps)
            device = (ctx_of(z_of(gi), y, core), to)
            remote(
                kvst.at[w, to], kv.at[z, y, w, own_rows], zt_s.at[w, gi], zt_r.at[w, z], device
            ).start()
    landed(qs.at[0], loc.at[2])
    q_copy = remote(qs.at[0], qs.at[1], pair_s.at[0], pair_r.at[0], dev_pair)
    q_copy.start()
    landed(gs.at[0], loc.at[3])
    g_copy = remote(gs.at[0], gs.at[1], pair_s.at[1], pair_r.at[1], dev_pair)
    g_copy.start()

    def spans(cc):
        s0, s1 = span[2 * cc], span[2 * cc + 1]
        return s0 > s1, jnp.minimum(s0, s1)

    devs = (c, ctx_of(z, y, 1 - core))
    flips, lows = zip(*[spans(d) for d in devs])

    def prepare(a, src, normal, turned):
        first = src[a, :, 0:SPAN, :].reshape(rows, HEAD)
        second = src[a, :, SPAN : 2 * SPAN, :].reshape(rows, HEAD)
        lo = jnp.where(flips[a], second, first)
        hi = jnp.where(flips[a], first, second)
        normal[a, :, 0:HEAD] = lo
        normal[a, :, HEAD : 2 * HEAD] = hi
        turned[a, 0:HEAD, :] = lo.T
        turned[a, HEAD : 2 * HEAD, :] = hi.T

    low, high = pl.ds(0, SPAN), pl.ds(SPAN, SPAN)

    def y_send(w, gi):
        zg = z_of(gi)
        b = kv.at[zg, y, w]
        landed(b, zt_r.at[w, zg])
        remote(b, b, ysem_s.at[w, gi, 0], ysem_r.at[w, gi, 0], dev_yu).start()
        remote(b, b, ysem_s.at[w, gi, 1], ysem_r.at[w, gi, 1], dev_yd).start()
        if (w, gi) not in AG_RELAY:
            remote(b, b, ysem_s.at[w, gi, 2], ysem_r.at[w, gi, 2], dev_yo).start()

    def y_relay(w, gi):
        zg = z_of(gi)
        landed(kv.at[zg, y_dn, w], ysem_r.at[w, gi, 0])
        b = kv.at[zg, y_dn, w, low]
        remote(b, b, ysem_s.at[w, gi, 2], ysem_r.at[w, gi, 2], dev_yu).start()
        landed(kv.at[zg, y_up, w], ysem_r.at[w, gi, 1])
        b = kv.at[zg, y_up, w, high]
        remote(b, b, ysem_s.at[w, gi, 3], ysem_r.at[w, gi, 3], dev_yd).start()

    def y_done(w, gi):
        zg = z_of(gi)
        if (w, gi) in AG_RELAY:
            landed(kv.at[zg, y_op, w, low], ysem_r.at[w, gi, 2])
            landed(kv.at[zg, y_op, w, high], ysem_r.at[w, gi, 3])
        else:
            landed(kv.at[zg, y_dn, w], ysem_r.at[w, gi, 0])
            landed(kv.at[zg, y_up, w], ysem_r.at[w, gi, 1])
            landed(kv.at[zg, y_op, w], ysem_r.at[w, gi, 2])

    def at(gi, todo):
        for g in range(NZ):
            pl.when(gi == g)(functools.partial(todo, g))

    y_send(0, 0)
    prepare(0, qs, qn, qt)
    y_send(0, 1)
    y_send(0, 2)

    def lohi(zg, yy, w):
        first, second = kv[zg, yy, w, 0:SPAN, :], kv[zg, yy, w, SPAN : 2 * SPAN, :]
        flip, _ = spans(ctx_of(zg, yy, core))
        return jnp.where(flip, second, first), jnp.where(flip, first, second)

    key_i = lax.broadcasted_iota(jnp.int32, (SPAN, rows), 0)
    tok_i = lax.rem(lax.broadcasted_iota(jnp.int32, (SPAN, rows), 1), SPAN)
    hidden = key_i > tok_i

    s3 = jnp.where(hidden, NEG, dot(lohi(z, y, 0)[0], qt[0, 0:HEAD, :]))
    s3_s[...] = s3
    m3 = jnp.max(s3, axis=0, keepdims=True)
    e3 = jnp.exp2((s3 - m3) * EXPO)
    none = jnp.full((1, rows), NEG, F32)
    zero = jnp.zeros((1, rows), F32)
    for a in range(2):
        st[a, 0:1, :] = none if a else m3
        st[a, 1:2, :] = zero if a else jnp.sum(e3, axis=0, keepdims=True)
        st[a, 2:3, :] = none
        st[a, 3:8, :] = jnp.zeros((5, rows), F32)
    y_send(0, 3)
    y_send(1, 0)
    prepare(0, gs, gn, gt)
    d3_s[...] = dot(lohi(z, y, 1)[0], gt[0, 0:HEAD, :])
    q_copy.wait_recv()
    prepare(1, qs, qn, qt)
    y_send(1, 1)
    y_send(1, 2)
    y_send(1, 3)

    def picks(zg, a):
        return [spans(ctx_of(zg, yy, core))[1] < lows[a] for yy in range(NY)]

    def block(yy):
        return slice(yy * SPAN, (yy + 1) * SPAN)

    def split(zg, w, lo_s, cat_s, gi):
        pairs = [lohi(zg, yy, w) for yy in range(NY)]
        for yy in range(NY):
            lo_s[gi, block(yy), :] = pairs[yy][0]
        for a in range(2):
            pick = picks(zg, a)
            for yy in range(NY):
                lo, hi = pairs[yy]
                none_ = jnp.zeros_like(lo)
                cat_s[gi, a, block(yy), 0:HEAD] = jnp.where(pick[yy], lo, none_)
                cat_s[gi, a, block(yy), HEAD : 2 * HEAD] = jnp.where(pick[yy], none_, hi)

    def column_sum(x):
        return jnp.sum(x, axis=0, keepdims=True)

    def scores(gi):
        zg = z_of(gi)
        split(zg, 0, klo_s, kc_s, gi)
        for a in range(2):
            pick = picks(zg, a)
            s1 = dot(klo_s[gi], qt[a, HEAD : 2 * HEAD, :])
            s2 = dot(kc_s[gi, a], qt[a])
            s_s[gi, a, 0] = s1
            parts = []
            for yy in range(NY):
                part = s2[block(yy), :]
                if a == 0:
                    here = jnp.logical_and(zg == z, yy == y)
                    part = jnp.where(jnp.logical_and(hidden, here), NEG, part)
                s_s[gi, a, 1, block(yy), :] = part
                parts.append(part)
            m_lo, l_lo, m_hi, l_hi = (st[a, i : i + 1, :] for i in range(4))
            n_lo, n_hi = m_lo, jnp.maximum(m_hi, jnp.max(s1, axis=0, keepdims=True))
            for yy in range(NY):
                top = jnp.max(parts[yy], axis=0, keepdims=True)
                n_lo = jnp.maximum(n_lo, jnp.where(pick[yy], top, none))
                n_hi = jnp.maximum(n_hi, jnp.where(pick[yy], none, top))
            l_lo = l_lo * jnp.exp2((m_lo - n_lo) * EXPO)
            l_hi = l_hi * jnp.exp2((m_hi - n_hi) * EXPO)
            l_hi = l_hi + column_sum(jnp.exp2((s1 - n_hi) * EXPO))
            for yy in range(NY):
                e2 = jnp.exp2((parts[yy] - jnp.where(pick[yy], n_lo, n_hi)) * EXPO)
                total = column_sum(e2)
                l_lo = l_lo + jnp.where(pick[yy], total, zero)
                l_hi = l_hi + jnp.where(pick[yy], zero, total)
            for i, x in enumerate((n_lo, l_lo, n_hi, l_hi)):
                st[a, i : i + 1, :] = x

    def score_step(gi, carry):
        at(gi, functools.partial(y_done, 0))
        scores(gi)
        return carry

    lax.fori_loop(0, NZ, score_step, 0)

    st_copy = remote(st, st_in, pair_s.at[2], pair_r.at[2], dev_pair)
    st_copy.start()
    dqt[...] = jnp.zeros_like(dqt)
    g_copy.wait_recv()
    prepare(1, gs, gn, gt)
    st_copy.wait_recv()
    for a in range(2):
        for at_ in (0, 2):
            m0, l0 = (st[a, at_ + i : at_ + i + 1, :] for i in range(2))
            m1, l1 = (st_in[1 - a, at_ + i : at_ + i + 1, :] for i in range(2))
            m = jnp.maximum(m0, m1)
            total = l0 * jnp.exp2((m0 - m) * EXPO) + l1 * jnp.exp2((m1 - m) * EXPO)
            cs[a, at_ : at_ + 1, :] = m
            cs[a, at_ + 1 : at_ + 2, :] = 1.0 / total

    def prob_of(s, m, inv):
        return jnp.exp2((s - m) * EXPO) * inv

    p3 = prob_of(s3_s[...], cs[0, 0:1, :], cs[0, 1:2, :])
    s3_s[...] = p3
    dk3[1] = dot(p3.astype(BF16), gn[0, :, 0:HEAD])
    for a in range(2):
        dl[a, 0:1, :] = zero if a else column_sum(p3 * d3_s[...])
        dl[a, 1:8, :] = jnp.zeros((7, rows), F32)

    def collect(gi, w, tiles, wide):
        zg = z_of(gi)
        dlo, dhi = [None] * NY, [None] * NY
        for a in range(2):
            x1, x2 = tiles(a)
            pick = picks(zg, a)
            one = dot(x1, wide[a, :, HEAD : 2 * HEAD])
            two = dot(x2, wide[a])
            for yy in range(NY):
                left, right = two[block(yy), 0:HEAD], two[block(yy), HEAD : 2 * HEAD]
                none_ = jnp.zeros_like(left)
                new_lo = one[block(yy), :] + jnp.where(pick[yy], left, none_)
                new_hi = jnp.where(pick[yy], none_, right)
                if a == 0:
                    here = jnp.logical_and(zg == z, yy == y)
                    dlo[yy], dhi[yy] = new_lo + jnp.where(here, dk3[w], none_), new_hi
                else:
                    dlo[yy], dhi[yy] = dlo[yy] + new_lo, dhi[yy] + new_hi
        for yy in range(NY):
            flip, _ = spans(ctx_of(zg, yy, core))
            out[zg, yy, w, 0:SPAN, :] = jnp.where(flip, dhi[yy], dlo[yy]).astype(BF16)
            out[zg, yy, w, SPAN : 2 * SPAN, :] = jnp.where(flip, dlo[yy], dhi[yy]).astype(BF16)

    def value_grads(gi):
        zg = z_of(gi)
        split(zg, 1, vlo_s, vc_s, gi)

        def tiles(a):
            pick = picks(zg, a)
            m_lo, i_lo, m_hi, i_hi = (cs[a, i : i + 1, :] for i in range(4))
            d1 = dot(vlo_s[gi], gt[a, HEAD : 2 * HEAD, :])
            d2 = dot(vc_s[gi, a], gt[a])
            d_s[gi, a, 0] = d1
            d_s[gi, a, 1] = d2
            p1 = prob_of(s_s[gi, a, 0], m_hi, i_hi)
            s_s[gi, a, 0] = p1
            e_lo, e_hi = dl[a, 0:1, :], dl[a, 1:2, :] + column_sum(p1 * d1)
            w2 = []
            for yy in range(NY):
                p2 = prob_of(
                    s_s[gi, a, 1, block(yy), :],
                    jnp.where(pick[yy], m_lo, m_hi),
                    jnp.where(pick[yy], i_lo, i_hi),
                )
                s_s[gi, a, 1, block(yy), :] = p2
                inner = column_sum(p2 * d2[block(yy), :])
                e_lo = e_lo + jnp.where(pick[yy], inner, zero)
                e_hi = e_hi + jnp.where(pick[yy], zero, inner)
                w2.append(p2.astype(BF16))
            dl[a, 0:1, :] = e_lo
            dl[a, 1:2, :] = e_hi
            return p1.astype(BF16), jnp.concatenate(w2, axis=0)

        collect(gi, 1, tiles, gn)
        klot_s[gi] = klo_s[gi].T
        for a in range(2):
            kct_s[gi, a] = kc_s[gi, a].T

    def score_grad(p, d, delta):
        return (p * (d - delta) * SCALE).astype(BF16)

    def key_grads(gi):
        zg = z_of(gi)

        def tiles(a):
            pick = picks(zg, a)
            e_lo, e_hi = (dl[a, i : i + 1, :] + dl_in[1 - a, i : i + 1, :] for i in range(2))
            ds1 = score_grad(s_s[gi, a, 0], d_s[gi, a, 0], e_hi)
            ds2 = jnp.concatenate(
                [
                    score_grad(
                        s_s[gi, a, 1, block(yy), :],
                        d_s[gi, a, 1, block(yy), :],
                        jnp.where(pick[yy], e_lo, e_hi),
                    )
                    for yy in range(NY)
                ],
                axis=0,
            )
            dqt[a] += dot(kct_s[gi, a], ds2)
            dqt[a, HEAD : 2 * HEAD, :] += dot(klot_s[gi], ds1)
            return ds1, ds2

        collect(gi, 0, tiles, qn)

    def plus(a, b):
        return (a.astype(F32) + b.astype(F32)).astype(BF16)

    def ry_first(w, gi):
        zg = z_of(gi)
        if (w, gi) in RS_RELAY:
            remote(
                out.at[zg, y_op, w, low], ro.at[gi, w, low], yo_s.at[w, gi, 0], yo_r.at[w, gi, 0], dev_yu
            ).start()
            remote(
                out.at[zg, y_op, w, high], ro.at[gi, w, high], yo_s.at[w, gi, 1], yo_r.at[w, gi, 1], dev_yd
            ).start()
        else:
            ry_near(w, gi, 0)
            ry_near(w, gi, 1)
            remote(
                out.at[zg, y_op, w], ro.at[gi, w], yo_s.at[w, gi, 0], yo_r.at[w, gi, 0], dev_yo
            ).start()

    def ry_near(w, gi, i):
        b = out.at[z_of(gi), (y_up, y_dn)[i], w]
        remote(
            b, ry.at[gi, i, w], yf_s.at[w, gi, i], yf_r.at[w, gi, i], (dev_yu, dev_yd)[i]
        ).start()

    def ry_forward(w, gi):
        zg = z_of(gi)
        landed(ro.at[gi, w, low], yo_r.at[w, gi, 0])
        out[zg, y_up, w, low] = plus(out[zg, y_up, w, low], ro[gi, w, low])
        ry_near(w, gi, 0)
        landed(ro.at[gi, w, high], yo_r.at[w, gi, 1])
        out[zg, y_dn, w, high] = plus(out[zg, y_dn, w, high], ro[gi, w, high])
        ry_near(w, gi, 1)

    def ry_total(w, gi):
        zg = z_of(gi)
        landed(ry.at[gi, 0, w], yf_r.at[w, gi, 0])
        landed(ry.at[gi, 1, w], yf_r.at[w, gi, 1])
        total = out[zg, y, w].astype(F32) + ry[gi, 0, w].astype(F32) + ry[gi, 1, w].astype(F32)
        if (w, gi) not in RS_RELAY:
            landed(ro.at[gi, w], yo_r.at[w, gi, 0])
            total = total + ro[gi, w].astype(F32)
        zs[gi, w] = total.astype(BF16)
        for o in range(1 if gi == 0 else 0, tps):
            to = lax.rem(t + o, tps)
            to_rows = pl.ds(pl.multiple_of(to * tt, tt), tt)
            device = (ctx_of(zg, y, core), to)
            remote(
                zs.at[gi, w, to_rows], kvr.at[z, w, t], zr_s.at[w, gi], zr_r.at[w, z], device
            ).start()

    def value_step(gi, carry):
        at(gi, functools.partial(y_done, 1))
        value_grads(gi)
        at(gi, functools.partial(ry_first, 1))
        return carry

    lax.fori_loop(0, NZ, value_step, 0)

    dl_copy = remote(dl, dl_in, pair_s.at[4], pair_r.at[4], dev_pair)
    dl_copy.start()
    dl_copy.wait_recv()
    ds3 = score_grad(s3_s[...], d3_s[...], dl[0, 0:1, :] + dl_in[1, 0:1, :])
    dk3[0] = dot(ds3, qn[0, :, 0:HEAD])
    dqt[0, 0:HEAD, :] = dot(lohi(z, y, 0)[0].T, ds3)

    def key_step(i, carry):
        gi = NZ - 1 - i
        key_grads(gi)
        at(gi, functools.partial(ry_first, 0))
        return carry

    lax.fori_loop(0, NZ, key_step, 0)

    dqsend[...] = dqt[1].astype(BF16)
    for gi in range(NZ - 1, -1, -1):
        ry_total(1, gi)
    dq_copy = remote(dqsend, dqrecv, pair_s.at[3], pair_r.at[3], dev_pair)
    dq_copy.start()
    kvr[z, 1, t] = zs[0, 1, own_rows]
    ry_total(0, 3)
    dq_copy.wait_recv()
    total_q = dqt[0] + dqrecv[...].astype(F32)
    lo, hi = total_q[0:HEAD, :].T.astype(BF16), total_q[HEAD : 2 * HEAD, :].T.astype(BF16)
    first, second = jnp.where(flips[0], hi, lo), jnp.where(flips[0], lo, hi)
    for h in range(heads):
        dqo[0:SPAN, h * HEAD : (h + 1) * HEAD] = first[h * SPAN : (h + 1) * SPAN, :]
        dqo[SPAN : 2 * SPAN, h * HEAD : (h + 1) * HEAD] = second[h * SPAN : (h + 1) * SPAN, :]
    ry_total(0, 2)
    results = [pltpu.make_async_copy(dqo, dq_out, loc.at[0])]
    results[0].start()
    ry_total(0, 1)
    ry_total(0, 0)
    kvr[z, 0, t] = zs[0, 0, own_rows]

    for copy in (q_copy, g_copy, st_copy, dl_copy, dq_copy):
        copy.wait_send()
    whole = kv.at[0, 0, 0]
    half = kv.at[0, 0, 0, low]
    pieces = [kvst.at[0, pl.ds(0, tps - 1)]] + [kvst.at[0]] * (NZ - 1)
    for w in range(2):
        for gi in range(NZ):
            landed(pieces[gi], zt_s.at[w, gi])
            landed(pieces[gi], zr_s.at[w, gi])
            relay = (w, gi) in AG_RELAY
            for i in range(4 if relay else 3):
                landed(half if relay and i >= 2 else whole, ysem_s.at[w, gi, i])
            relay = (w, gi) in RS_RELAY
            for i in range(2 if relay else 1):
                landed(half if relay else whole, yo_s.at[w, gi, i])
            for i in range(2):
                landed(whole, yf_s.at[w, gi, i])
    for w, result in ((1, v_out), (0, k_out)):
        for gi in range(NZ - 1, -1, -1):
            landed(pieces[gi], zr_r.at[w, z_of(gi)])
        for g in range(tps):
            total = kvr[0, w, g].astype(F32)
            for i in range(1, NZ):
                total = total + kvr[i, w, g].astype(F32)
            kvo[w, :, g * HEAD : (g + 1) * HEAD] = total.astype(BF16)
        results.append(pltpu.make_async_copy(kvo.at[w], result, loc.at[1 + w]))
        results[-1].start()
    for copy in results:
        copy.wait()


def body(queries, keys, values, output_gradient, span_order):
    tps = lax.axis_size("tp")
    toks, width = queries.shape
    heads = width // HEAD
    rows = heads * SPAN
    tt = keys.shape[0]
    vmem = pltpu.VMEM
    half = (toks, HEAD)
    block = (2, *half)
    group = NY * SPAN
    dma = pltpu.SemaphoreType.DMA
    scratch = [
        vmem((2, tps, tt, HEAD), BF16),
        vmem((NZ, NY, *block), BF16),
        vmem((2, heads, *half), BF16),
        vmem((2, heads, *half), BF16),
        vmem((2, rows, 2 * HEAD), BF16),
        vmem((2, rows, 2 * HEAD), BF16),
        vmem((2, 2 * HEAD, rows), BF16),
        vmem((2, 2 * HEAD, rows), BF16),
        vmem((NZ, group, HEAD), BF16),
        vmem((NZ, 2, group, 2 * HEAD), BF16),
        vmem((NZ, HEAD, group), BF16),
        vmem((NZ, 2, 2 * HEAD, group), BF16),
        vmem((NZ, group, HEAD), BF16),
        vmem((NZ, 2, group, 2 * HEAD), BF16),
        vmem((NZ, 2, 2, group, rows), F32),
        vmem((NZ, 2, 2, group, rows), F32),
        vmem((SPAN, rows), F32),
        vmem((SPAN, rows), F32),
        vmem((2, 8, rows), F32),
        vmem((2, 8, rows), F32),
        vmem((2, 8, rows), F32),
        vmem((2, 8, rows), F32),
        vmem((2, 8, rows), F32),
        vmem((2, 2 * HEAD, rows), F32),
        vmem((2, SPAN, HEAD), F32),
        vmem((2 * HEAD, rows), BF16),
        vmem((2 * HEAD, rows), BF16),
        vmem((NZ, NY, *block), BF16),
        vmem((NZ, *block), BF16),
        vmem((NZ, 2, *block), BF16),
        vmem((NZ, *block), BF16),
        vmem((NZ, 2, tps, tt, HEAD), BF16),
        vmem(queries.shape, BF16),
        vmem((2, *keys.shape), BF16),
        dma((4,)),
        dma((2, NZ)),
        dma((2, NZ)),
        dma((2, NZ, 4)),
        dma((2, NZ, 4)),
        dma((5,)),
        dma((5,)),
        dma((2, NZ, 2)),
        dma((2, NZ, 2)),
        dma((2, NZ, 2)),
        dma((2, NZ, 2)),
        dma((2, NZ)),
        dma((2, NZ)),
    ]
    anywhere = pl.BlockSpec(memory_space=pl.ANY)
    return tuple(
        pl.pallas_call(
            functools.partial(kernel, tps, heads),
            out_shape=(
                jax.ShapeDtypeStruct(queries.shape, BF16),
                jax.ShapeDtypeStruct(keys.shape, BF16),
                jax.ShapeDtypeStruct(values.shape, BF16),
            ),
            in_specs=[pl.BlockSpec(memory_space=pltpu.SMEM)] + [anywhere] * 4,
            out_specs=(anywhere,) * 3,
            scratch_shapes=scratch,
            compiler_params=pltpu.CompilerParams(
                collective_id=0, has_side_effects=True, vmem_limit_bytes=56 * 1024 * 1024
            ),
        )(span_order, queries, keys, values, output_gradient)
    )


def solution(mesh):
    return jax.shard_map(
        body,
        mesh=mesh,
        in_specs=(
            P("ctx", "tp"),
            P(("ctx", "tp"), None),
            P(("ctx", "tp"), None),
            P("ctx", "tp"),
            P(),
        ),
        out_specs=(P("ctx", "tp"), P(("ctx", "tp"), None), P(("ctx", "tp"), None)),
        check_vma=False,
    )
```

time: 62 us -> 53.4 us (0.86)
  the two profiles are of different devices: /device:TPU:32 before, /device:TPU:1 now
where the time goes in v2:
time: 53.4 us; the launch traced here: 53.1 us
  Pallas kernels  49.4 us (93%)
  local copies, waits for them, and re-layouts  3.06 us (6%)
  between operations  0.65 us (1%)
    pallas_call x1, Pallas kernels, body(): pl.pallas_call(functools.partial(kernel, tps, heads), out_shape=(jax.Shap...  49.4 us
    unnamed x7, local copies, waits for them, and re-layouts  3.06 us

profile of v2, /device:TPU:1, one launch (start us, length us, event | category | flops | bytes accessed | tf_op | source)
XLA Modules:
  0.0 53.1 jit_solution(17856068517534169395)
XLA Ops:
  0.6 49.4 %shard_map.76 = (bf16[128,1024]{1,0:T(8,128)(2,1)}, bf16[16,1024]{1,0:T(8,128)(2,1)}, bf16[16,1024]{1,0:T(8,128)(2,1)}) custom-call(s32[64]{0:T(128)} %span.1, bf16[128,1024]{1,0:T(8,128)(2,1)} %q_hbm.1, bf16[16,1024]{1,0:T(8,128)(2,1)} %k_hbm.1, bf16[16,1024]{1,0:T(8,128)(2,1)} %v_hbm.1, bf16[128,1024]{1,0:T(8,128)(2,1)} %g_hbm.1), custom_call_target="tpu_custom_call" | custom-call | tf_op jit(solution)/shard_map/pallas_call | solution.py:609
  50.1 0.0 copy-start.1
  50.1 1.7 %copy.11 = bf16[128,1024]{1,0:T(8,128)(2,1)} copy(bf16[128,1024]{1,0:T(8,128)(2,1)} %get-tuple-element.6) | data formatting | bytes 524288
  51.8 0.0 copy-done.1
  51.8 0.0 copy-start
  51.8 0.6 %copy.12 = bf16[16,1024]{1,0:T(8,128)(2,1)} copy(bf16[16,1024]{1,0:T(8,128)(2,1)S(1)} %copy-done.1) | data formatting | bytes 65536
  52.4 0.2 copy-done
  52.5 0.6 %copy.13 = bf16[16,1024]{1,0:T(8,128)(2,1)} copy(bf16[16,1024]{1,0:T(8,128)(2,1)S(1)} %copy-done) | data formatting | bytes 65536
Async XLA Ops:
  50.1 1.7 %copy-start.1 = (bf16[16,1024]{1,0:T(8,128)(2,1)S(1)}, bf16[16,1024]{1,0:T(8,128)(2,1)}, u32[]{:S(2)}) copy-start(bf16[16,1024]{1,0:T(8,128)(2,1)} %get-tuple-element.7) | copy-start | bytes 98308
  51.8 0.8 %copy-start = (bf16[16,1024]{1,0:T(8,128)(2,1)S(1)}, bf16[16,1024]{1,0:T(8,128)(2,1)}, u32[]{:S(2)}) copy-start(bf16[16,1024]{1,0:T(8,128)(2,1)} %get-tuple-element.8) | copy-start | bytes 98308

commit v3 on v2

--- a/solution.py
+++ b/solution.py
@@ -16,8 +16,12 @@
 SCALE = HEAD**-0.5
 EXPO = SCALE * math.log2(math.e)
 NEG = -1e30
+ZT_FIRST = ((0, 0), (1, 0), (0, 1), (0, 2), (0, 3), (1, 1), (1, 2), (1, 3))
 AG_RELAY = ()
+INNER_AHEAD = 1
+Z_FIRST = ()
 RS_RELAY = ()
+POINTS = {'first': (('send', 1, 0),), 'second': (), 'third': (), 'score': {0: (('send', 1, 1),), 1: (('send', 1, 2),), 2: (('send', 1, 3),)}, 'stats': (('inner', 1, 0),), 'delta': (), 'key': {2: (('total', 1, 1),), 3: (('total', 1, 2),)}, 'keys': (), 'last': (('total', 1, 3), ('total', 1, 0), ('total', 0, 3), ('total', 0, 2)), 'end': (('total', 0, 1), ('total', 0, 0)), 'value': {}}
 MESH = pl.DeviceIdType.MESH
 F32 = jnp.float32
 BF16 = jnp.bfloat16
@@ -48,12 +52,11 @@
     gt,
     klo_s,
     kc_s,
-    klot_s,
-    kct_s,
     vlo_s,
     vc_s,
     s_s,
     d_s,
+    ds_s,
     s3_s,
     d3_s,
     st,
@@ -70,8 +73,7 @@
     ry,
     zs,
     kvr,
-    dqo,
-    kvo,
+    rzv,
     loc,
     zt_s,
     zt_r,
@@ -85,6 +87,8 @@
     yf_r,
     zr_s,
     zr_r,
+    zv_s,
+    zv_r,
 ):
     rows = heads * SPAN
     toks = 2 * SPAN
@@ -118,7 +122,8 @@
 
     own_rows = pl.ds(pl.multiple_of(t * tt, tt), tt)
     own_cols = pl.ds(pl.multiple_of(t * HEAD, HEAD), HEAD)
-    for w, hbm in enumerate((k_hbm, v_hbm)):
+
+    def fetch(w, hbm):
         for g in range(tps):
             pltpu.make_async_copy(
                 hbm.at[:, pl.ds(g * HEAD, HEAD)], kvst.at[w, g], loc.at[w]
@@ -126,10 +131,8 @@
         pltpu.make_async_copy(
             hbm.at[:, own_cols], kv.at[z, y, w, own_rows], zt_r.at[w, z]
         ).start()
-    for h in range(heads):
-        cols = pl.ds(h * HEAD, HEAD)
-        pltpu.make_async_copy(q_hbm.at[:, cols], qs.at[0, h], loc.at[2]).start()
-        pltpu.make_async_copy(g_hbm.at[:, cols], gs.at[0, h], loc.at[3]).start()
+
+    fetch(0, k_hbm)
 
     def z_of(gi):
         return lax.rem(z + gi + (gi // 2) * (1 - 2 * (gi % 2)), NZ)
@@ -143,17 +146,25 @@
             greet((ctx_of(z_of(gi), y, core), lax.rem(t + o, tps)))
     for device in (dev_yu, dev_yd, dev_yo, dev_pair):
         greet(device)
+    fetch(1, v_hbm)
     landed(kvst.at[0], loc.at[0])
     landed(kvst.at[1], loc.at[1])
     pl.semaphore_wait(barrier, NZ * tps - 1 + 4)
 
-    for w, gi in ((0, 0), (1, 0), (0, 1), (0, 2), (0, 3), (1, 1), (1, 2), (1, 3)):
+    def zt_send(w, gi):
         for o in range(1 if gi == 0 else 0, tps):
             to = lax.rem(t + o, tps)
             device = (ctx_of(z_of(gi), y, core), to)
             remote(
                 kvst.at[w, to], kv.at[z, y, w, own_rows], zt_s.at[w, gi], zt_r.at[w, z], device
             ).start()
+
+    for w, gi in ZT_FIRST:
+        zt_send(w, gi)
+    for h in range(heads):
+        cols = pl.ds(h * HEAD, HEAD)
+        pltpu.make_async_copy(q_hbm.at[:, cols], qs.at[0, h], loc.at[2]).start()
+        pltpu.make_async_copy(g_hbm.at[:, cols], gs.at[0, h], loc.at[3]).start()
     landed(qs.at[0], loc.at[2])
     q_copy = remote(qs.at[0], qs.at[1], pair_s.at[0], pair_r.at[0], dev_pair)
     q_copy.start()
@@ -208,14 +219,28 @@
             landed(kv.at[zg, y_up, w], ysem_r.at[w, gi, 1])
             landed(kv.at[zg, y_op, w], ysem_r.at[w, gi, 2])
 
+    steps = {}
+
+    def act(name, g=None):
+        for step, w, gi in POINTS[name] if g is None else POINTS[name].get(g, ()):
+            steps[step](w, gi)
+
+    def point(name, i):
+        for g in POINTS[name]:
+            pl.when(i == g)(functools.partial(act, name, g))
+
     def at(gi, todo):
         for g in range(NZ):
             pl.when(gi == g)(functools.partial(todo, g))
 
+    steps["relay"], steps["send"] = y_relay, y_send
     y_send(0, 0)
     prepare(0, qs, qn, qt)
+    steps["zt"] = zt_send
+    act("first")
     y_send(0, 1)
     y_send(0, 2)
+    act("second")
 
     def lohi(zg, yy, w):
         first, second = kv[zg, yy, w, 0:SPAN, :], kv[zg, yy, w, SPAN : 2 * SPAN, :]
@@ -238,15 +263,10 @@
         st[a, 2:3, :] = none
         st[a, 3:8, :] = jnp.zeros((5, rows), F32)
     y_send(0, 3)
-    y_send(1, 0)
+    act("third")
     prepare(0, gs, gn, gt)
-    d3_s[...] = dot(lohi(z, y, 1)[0], gt[0, 0:HEAD, :])
     q_copy.wait_recv()
     prepare(1, qs, qn, qt)
-    y_send(1, 1)
-    y_send(1, 2)
-    y_send(1, 3)
-
     def picks(zg, a):
         return [spans(ctx_of(zg, yy, core))[1] < lows[a] for yy in range(NY)]
 
@@ -301,9 +321,22 @@
             for i, x in enumerate((n_lo, l_lo, n_hi, l_hi)):
                 st[a, i : i + 1, :] = x
 
+    def inner(gi):
+        split(z_of(gi), 1, vlo_s, vc_s, gi)
+        for a in range(2):
+            d_s[gi, a, 0] = dot(vlo_s[gi], gt[a, HEAD : 2 * HEAD, :])
+            d_s[gi, a, 1] = dot(vc_s[gi, a], gt[a])
+
+    def inner_now(w, gi):
+        y_done(w, gi)
+        inner(gi)
+
+    steps["inner"] = inner_now
+
     def score_step(gi, carry):
         at(gi, functools.partial(y_done, 0))
         scores(gi)
+        point("score", gi)
         return carry
 
     lax.fori_loop(0, NZ, score_step, 0)
@@ -313,6 +346,7 @@
     dqt[...] = jnp.zeros_like(dqt)
     g_copy.wait_recv()
     prepare(1, gs, gn, gt)
+    act("stats")
     st_copy.wait_recv()
     for a in range(2):
         for at_ in (0, 2):
@@ -326,6 +360,7 @@
     def prob_of(s, m, inv):
         return jnp.exp2((s - m) * EXPO) * inv
 
+    d3_s[...] = dot(lohi(z, y, 1)[0], gt[0, 0:HEAD, :])
     p3 = prob_of(s3_s[...], cs[0, 0:1, :], cs[0, 1:2, :])
     s3_s[...] = p3
     dk3[1] = dot(p3.astype(BF16), gn[0, :, 0:HEAD])
@@ -358,18 +393,12 @@
 
     def value_grads(gi):
         zg = z_of(gi)
-        split(zg, 1, vlo_s, vc_s, gi)
 
         def tiles(a):
             pick = picks(zg, a)
             m_lo, i_lo, m_hi, i_hi = (cs[a, i : i + 1, :] for i in range(4))
-            d1 = dot(vlo_s[gi], gt[a, HEAD : 2 * HEAD, :])
-            d2 = dot(vc_s[gi, a], gt[a])
-            d_s[gi, a, 0] = d1
-            d_s[gi, a, 1] = d2
             p1 = prob_of(s_s[gi, a, 0], m_hi, i_hi)
             s_s[gi, a, 0] = p1
-            e_lo, e_hi = dl[a, 0:1, :], dl[a, 1:2, :] + column_sum(p1 * d1)
             w2 = []
             for yy in range(NY):
                 p2 = prob_of(
@@ -378,18 +407,23 @@
                     jnp.where(pick[yy], i_lo, i_hi),
                 )
                 s_s[gi, a, 1, block(yy), :] = p2
-                inner = column_sum(p2 * d2[block(yy), :])
-                e_lo = e_lo + jnp.where(pick[yy], inner, zero)
-                e_hi = e_hi + jnp.where(pick[yy], zero, inner)
                 w2.append(p2.astype(BF16))
+            return p1.astype(BF16), jnp.concatenate(w2, axis=0)
+
+        collect(gi, 1, tiles, gn)
+
+    def deltas(gi):
+        zg = z_of(gi)
+        for a in range(2):
+            pick = picks(zg, a)
+            e_lo = dl[a, 0:1, :]
+            e_hi = dl[a, 1:2, :] + column_sum(s_s[gi, a, 0] * d_s[gi, a, 0])
+            for yy in range(NY):
+                part = column_sum(s_s[gi, a, 1, block(yy), :] * d_s[gi, a, 1, block(yy), :])
+                e_lo = e_lo + jnp.where(pick[yy], part, zero)
+                e_hi = e_hi + jnp.where(pick[yy], zero, part)
             dl[a, 0:1, :] = e_lo
             dl[a, 1:2, :] = e_hi
-            return p1.astype(BF16), jnp.concatenate(w2, axis=0)
-
-        collect(gi, 1, tiles, gn)
-        klot_s[gi] = klo_s[gi].T
-        for a in range(2):
-            kct_s[gi, a] = kc_s[gi, a].T
 
     def score_grad(p, d, delta):
         return (p * (d - delta) * SCALE).astype(BF16)
@@ -400,23 +434,22 @@
         def tiles(a):
             pick = picks(zg, a)
             e_lo, e_hi = (dl[a, i : i + 1, :] + dl_in[1 - a, i : i + 1, :] for i in range(2))
-            ds1 = score_grad(s_s[gi, a, 0], d_s[gi, a, 0], e_hi)
-            ds2 = jnp.concatenate(
-                [
-                    score_grad(
-                        s_s[gi, a, 1, block(yy), :],
-                        d_s[gi, a, 1, block(yy), :],
-                        jnp.where(pick[yy], e_lo, e_hi),
-                    )
-                    for yy in range(NY)
-                ],
-                axis=0,
-            )
-            dqt[a] += dot(kct_s[gi, a], ds2)
-            dqt[a, HEAD : 2 * HEAD, :] += dot(klot_s[gi], ds1)
-            return ds1, ds2
+            ds_s[gi, a, 0] = score_grad(s_s[gi, a, 0], d_s[gi, a, 0], e_hi)
+            for yy in range(NY):
+                ds_s[gi, a, 1, block(yy), :] = score_grad(
+                    s_s[gi, a, 1, block(yy), :],
+                    d_s[gi, a, 1, block(yy), :],
+                    jnp.where(pick[yy], e_lo, e_hi),
+                )
+            return ds_s[gi, a, 0], ds_s[gi, a, 1]
 
         collect(gi, 0, tiles, qn)
+
+    def query_step(gi, carry):
+        for a in range(2):
+            dqt[a] += dot(kc_s[gi, a].T, ds_s[gi, a, 1])
+            dqt[a, HEAD : 2 * HEAD, :] += dot(klo_s[gi].T, ds_s[gi, a, 0])
+        return carry
 
     def plus(a, b):
         return (a.astype(F32) + b.astype(F32)).astype(BF16)
@@ -469,16 +502,51 @@
                 zs.at[gi, w, to_rows], kvr.at[z, w, t], zr_s.at[w, gi], zr_r.at[w, z], device
             ).start()
 
-    def value_step(gi, carry):
-        at(gi, functools.partial(y_done, 1))
+    steps["forward"], steps["total"] = ry_forward, ry_total
+
+    def z_first(gi):
+        zg = z_of(gi)
+        remote(
+            out.at[zg, :, 1], rzv.at[gi - 1], zv_s.at[gi - 1], zv_r.at[gi - 1], (ctx_of(zg, y, core), t)
+        ).start()
+
+    def z_merge(w, gi):
+        for i in range(2):
+            landed(rzv.at[i], zv_r.at[i])
+        for yy in range(NY):
+            total = out[z, yy, w].astype(F32) + rzv[0, yy].astype(F32) + rzv[1, yy].astype(F32)
+            out[z, yy, w] = total.astype(BF16)
+        ry_first(w, gi)
+
+    steps["merge"] = z_merge
+
+    def value_step(i, carry):
+        gi = lax.rem(i + 1, NZ)
         value_grads(gi)
-        at(gi, functools.partial(ry_first, 1))
+        for g in range(1 if Z_FIRST else 0, NZ):
+            pl.when(gi == g)(
+                functools.partial(z_first, g) if g in Z_FIRST else functools.partial(ry_first, 1, g)
+            )
         return carry
 
     lax.fori_loop(0, NZ, value_step, 0)
+
+    def delta_step(gi, carry):
+        for g in range(INNER_AHEAD, NZ):
+            pl.when(gi == g)(functools.partial(y_done, 1, g))
+
+        @pl.when(gi >= INNER_AHEAD)
+        def _():
+            inner(gi)
+
+        deltas(gi)
+        return carry
+
+    lax.fori_loop(0, NZ, delta_step, 0)
 
     dl_copy = remote(dl, dl_in, pair_s.at[4], pair_r.at[4], dev_pair)
     dl_copy.start()
+    act("delta")
     dl_copy.wait_recv()
     ds3 = score_grad(s3_s[...], d3_s[...], dl[0, 0:1, :] + dl_in[1, 0:1, :])
     dk3[0] = dot(ds3, qn[0, :, 0:HEAD])
@@ -488,30 +556,27 @@
         gi = NZ - 1 - i
         key_grads(gi)
         at(gi, functools.partial(ry_first, 0))
+        point("key", i)
         return carry
 
     lax.fori_loop(0, NZ, key_step, 0)
 
+    act("keys")
+    lax.fori_loop(0, NZ, query_step, 0)
     dqsend[...] = dqt[1].astype(BF16)
-    for gi in range(NZ - 1, -1, -1):
-        ry_total(1, gi)
     dq_copy = remote(dqsend, dqrecv, pair_s.at[3], pair_r.at[3], dev_pair)
     dq_copy.start()
-    kvr[z, 1, t] = zs[0, 1, own_rows]
-    ry_total(0, 3)
+    act("last")
     dq_copy.wait_recv()
     total_q = dqt[0] + dqrecv[...].astype(F32)
     lo, hi = total_q[0:HEAD, :].T.astype(BF16), total_q[HEAD : 2 * HEAD, :].T.astype(BF16)
     first, second = jnp.where(flips[0], hi, lo), jnp.where(flips[0], lo, hi)
     for h in range(heads):
-        dqo[0:SPAN, h * HEAD : (h + 1) * HEAD] = first[h * SPAN : (h + 1) * SPAN, :]
-        dqo[SPAN : 2 * SPAN, h * HEAD : (h + 1) * HEAD] = second[h * SPAN : (h + 1) * SPAN, :]
-    ry_total(0, 2)
-    results = [pltpu.make_async_copy(dqo, dq_out, loc.at[0])]
-    results[0].start()
-    ry_total(0, 1)
-    ry_total(0, 0)
-    kvr[z, 0, t] = zs[0, 0, own_rows]
+        dq_out[0:SPAN, h * HEAD : (h + 1) * HEAD] = first[h * SPAN : (h + 1) * SPAN, :]
+        dq_out[SPAN : 2 * SPAN, h * HEAD : (h + 1) * HEAD] = second[h * SPAN : (h + 1) * SPAN, :]
+    act("end")
+    for w in range(2):
+        kvr[z, w, t] = zs[0, w, own_rows]
 
     for copy in (q_copy, g_copy, st_copy, dl_copy, dq_copy):
         copy.wait_send()
@@ -521,27 +586,28 @@
     for w in range(2):
         for gi in range(NZ):
             landed(pieces[gi], zt_s.at[w, gi])
-            landed(pieces[gi], zr_s.at[w, gi])
+            straight = w == 0 or gi not in Z_FIRST
+            if straight:
+                landed(pieces[gi], zr_s.at[w, gi])
             relay = (w, gi) in AG_RELAY
             for i in range(4 if relay else 3):
                 landed(half if relay and i >= 2 else whole, ysem_s.at[w, gi, i])
             relay = (w, gi) in RS_RELAY
             for i in range(2 if relay else 1):
-                landed(half if relay else whole, yo_s.at[w, gi, i])
+                if straight:
+                    landed(half if relay else whole, yo_s.at[w, gi, i])
             for i in range(2):
-                landed(whole, yf_s.at[w, gi, i])
+                if straight:
+                    landed(whole, yf_s.at[w, gi, i])
+    for i in range(len(Z_FIRST)):
+        landed(rzv.at[i], zv_s.at[i])
     for w, result in ((1, v_out), (0, k_out)):
-        for gi in range(NZ - 1, -1, -1):
+        parts = [gi for gi in (3, 2, 1, 0) if w == 0 or gi not in Z_FIRST]
+        for gi in parts:
             landed(pieces[gi], zr_r.at[w, z_of(gi)])
         for g in range(tps):
-            total = kvr[0, w, g].astype(F32)
-            for i in range(1, NZ):
-                total = total + kvr[i, w, g].astype(F32)
-            kvo[w, :, g * HEAD : (g + 1) * HEAD] = total.astype(BF16)
-        results.append(pltpu.make_async_copy(kvo.at[w], result, loc.at[1 + w]))
-        results[-1].start()
-    for copy in results:
-        copy.wait()
+            total = sum(kvr[z_of(gi), w, g].astype(F32) for gi in parts)
+            result[:, g * HEAD : (g + 1) * HEAD] = total.astype(BF16)
 
 
 def body(queries, keys, values, output_gradient, span_order):
@@ -566,12 +632,11 @@
         vmem((2, 2 * HEAD, rows), BF16),
         vmem((NZ, group, HEAD), BF16),
         vmem((NZ, 2, group, 2 * HEAD), BF16),
-        vmem((NZ, HEAD, group), BF16),
-        vmem((NZ, 2, 2 * HEAD, group), BF16),
         vmem((NZ, group, HEAD), BF16),
         vmem((NZ, 2, group, 2 * HEAD), BF16),
         vmem((NZ, 2, 2, group, rows), F32),
         vmem((NZ, 2, 2, group, rows), F32),
+        vmem((NZ, 2, 2, group, rows), BF16),
         vmem((SPAN, rows), F32),
         vmem((SPAN, rows), F32),
         vmem((2, 8, rows), F32),
@@ -588,8 +653,7 @@
         vmem((NZ, 2, *block), BF16),
         vmem((NZ, *block), BF16),
         vmem((NZ, 2, tps, tt, HEAD), BF16),
-        vmem(queries.shape, BF16),
-        vmem((2, *keys.shape), BF16),
+        vmem((2, NY, *half), BF16),
         dma((4,)),
         dma((2, NZ)),
         dma((2, NZ)),
@@ -603,24 +667,43 @@
         dma((2, NZ, 2)),
         dma((2, NZ)),
         dma((2, NZ)),
+        dma((2,)),
+        dma((2,)),
     ]
     anywhere = pl.BlockSpec(memory_space=pl.ANY)
+    in_vmem = pl.BlockSpec(memory_space=pltpu.VMEM)
+    shapes = (queries.shape, keys.shape, values.shape)
+    grads = pl.pallas_call(
+        functools.partial(kernel, tps, heads),
+        out_shape=tuple(pltpu.VMEM(shape, BF16) for shape in shapes),
+        in_specs=[pl.BlockSpec(memory_space=pltpu.SMEM)] + [anywhere] * 4,
+        out_specs=(in_vmem,) * 3,
+        scratch_shapes=scratch,
+        compiler_params=pltpu.CompilerParams(
+            collective_id=0, has_side_effects=True, vmem_limit_bytes=56 * 1024 * 1024
+        ),
+    )(span_order, queries, keys, values, output_gradient)
     return tuple(
         pl.pallas_call(
-            functools.partial(kernel, tps, heads),
-            out_shape=(
-                jax.ShapeDtypeStruct(queries.shape, BF16),
-                jax.ShapeDtypeStruct(keys.shape, BF16),
-                jax.ShapeDtypeStruct(values.shape, BF16),
-            ),
-            in_specs=[pl.BlockSpec(memory_space=pltpu.SMEM)] + [anywhere] * 4,
+            put_out,
+            out_shape=tuple(jax.ShapeDtypeStruct(shape, BF16) for shape in shapes),
+            in_specs=[in_vmem] * 3,
             out_specs=(anywhere,) * 3,
-            scratch_shapes=scratch,
-            compiler_params=pltpu.CompilerParams(
-                collective_id=0, has_side_effects=True, vmem_limit_bytes=56 * 1024 * 1024
-            ),
-        )(span_order, queries, keys, values, output_gradient)
+            scratch_shapes=[dma((3,))],
+            compiler_params=pltpu.CompilerParams(vmem_limit_bytes=2 * 1024 * 1024),
+        )(*grads)
     )
+
+
+def put_out(a, b, c, x, y, z, sems):
+    copies = [
+        pltpu.make_async_copy(src, dst, sems.at[i])
+        for i, (src, dst) in enumerate(((a, x), (b, y), (c, z)))
+    ]
+    for copy in copies:
+        copy.start()
+    for copy in copies:
+        copy.wait()
 
 
 def solution(mesh):

time: 53.4 us -> 50.2 us (0.940)
  local copies, waits for them, and re-layouts: 3.06 us -> 0 us
    unnamed x7 -> x0, local copies, waits for them, and re-layouts: 3.06 us -> none
    pallas_call x1 -> x2, Pallas kernels: 49.4 us -> 49.3 us  [the longest x1 48.6 us: body(): pl.pallas_call(functools.partial(kernel, tps, heads), out_shape=tuple((pl...]
where the time goes in v3:
time: 50.2 us; the launch traced here: 50 us
  Pallas kernels  49.3 us (98%)
  between operations  0.64 us (1%)
    pallas_call x1, Pallas kernels, body(): pl.pallas_call(functools.partial(kernel, tps, heads), out_shape=tuple((pl...  48.6 us

profile of v3, /device:TPU:1, one launch (start us, length us, event | category | flops | bytes accessed | tf_op | source)
XLA Modules:
  0.0 50.0 jit_solution(450121444142635025)
XLA Ops:
  0.6 48.6 %shard_map.76 = (bf16[128,1024]{1,0:T(8,128)(2,1)S(1)}, bf16[16,1024]{1,0:T(8,128)(2,1)S(1)}, bf16[16,1024]{1,0:T(8,128)(2,1)S(1)}) custom-call(s32[64]{0:T(128)} %span.1, bf16[128,1024]{1,0:T(8,128)(2,1)} %q_hbm.1, bf16[16,1024]{1,0:T(8,128)(2,1)} %k_hbm.1, bf16[16,1024]{1,0:T(8,128)(2,1)} %v_hbm.1, bf16[128,1024]{1,0:T(8,128)(2,1)} %g_hbm.1), custom_call_target="tpu_custom_call" | custom-call | tf_op jit(solution)/shard_map/pallas_call | solution.py:676
  49.2 0.7 %shard_map.77 = (bf16[128,1024]{1,0:T(8,128)(2,1)}, bf16[16,1024]{1,0:T(8,128)(2,1)}, bf16[16,1024]{1,0:T(8,128)(2,1)}) custom-call(bf16[128,1024]{1,0:T(8,128)(2,1)S(1)} %get-tuple-element.6.a, bf16[16,1024]{1,0:T(8,128)(2,1)S(1)} %get-tuple-element.7.b, bf16[16,1024]{1,0:T(8,128)(2,1)S(1)} %get-tuple-element.8.c), custom_call_target="tpu_custom_call" | custom-call | tf_op jit(solution)/shard_map/pallas_call | solution.py:687

commit v4 on v3

--- a/solution.py
+++ b/solution.py
@@ -16,12 +16,12 @@
 SCALE = HEAD**-0.5
 EXPO = SCALE * math.log2(math.e)
 NEG = -1e30
-ZT_FIRST = ((0, 0), (1, 0), (0, 1), (0, 2), (0, 3), (1, 1), (1, 2), (1, 3))
+ZT_FIRST = ((0, 0), (0, 1), (0, 2), (0, 3))
 AG_RELAY = ()
 INNER_AHEAD = 1
 Z_FIRST = ()
 RS_RELAY = ()
-POINTS = {'first': (('send', 1, 0),), 'second': (), 'third': (), 'score': {0: (('send', 1, 1),), 1: (('send', 1, 2),), 2: (('send', 1, 3),)}, 'stats': (('inner', 1, 0),), 'delta': (), 'key': {2: (('total', 1, 1),), 3: (('total', 1, 2),)}, 'keys': (), 'last': (('total', 1, 3), ('total', 1, 0), ('total', 0, 3), ('total', 0, 2)), 'end': (('total', 0, 1), ('total', 0, 0)), 'value': {}}
+POINTS = {'early': (('zt', 1, 0), ('zt', 1, 1, 0), ('zt', 1, 2, 0), ('zt', 1, 3, 0)), 'first': (('pair', 0, 0), ('send', 1, 0, 0)), 'second': (('pair', 1, 0),), 'third': (('zt', 1, 1, 1), ('zt', 1, 2, 1), ('zt', 1, 3, 1)), 'score': {0: (('send', 1, 1, 0), ('send', 1, 0, 1)), 1: (('send', 1, 2, 0),), 2: (('send', 1, 3, 0), ('send', 1, 1, 1)), 3: (('send', 1, 2, 1), ('send', 1, 3, 1))}, 'stats': (('inner', 1, 0),), 'value': {}, 'delta': (), 'key': {0: (('total', 1, 3),), 1: (('total', 1, 2),), 2: (('total', 1, 1),), 3: (('total', 1, 0),)}, 'keys': (), 'last': (('total', 0, 3), ('total', 0, 2)), 'end': (('total', 0, 1), ('total', 0, 0))}
 MESH = pl.DeviceIdType.MESH
 F32 = jnp.float32
 BF16 = jnp.bfloat16
@@ -148,10 +148,11 @@
         greet(device)
     fetch(1, v_hbm)
     landed(kvst.at[0], loc.at[0])
-    landed(kvst.at[1], loc.at[1])
     pl.semaphore_wait(barrier, NZ * tps - 1 + 4)
 
     def zt_send(w, gi):
+        if (w, gi) == (1, 0):
+            landed(kvst.at[1], loc.at[1])
         for o in range(1 if gi == 0 else 0, tps):
             to = lax.rem(t + o, tps)
             device = (ctx_of(z_of(gi), y, core), to)
@@ -165,12 +166,13 @@
         cols = pl.ds(h * HEAD, HEAD)
         pltpu.make_async_copy(q_hbm.at[:, cols], qs.at[0, h], loc.at[2]).start()
         pltpu.make_async_copy(g_hbm.at[:, cols], gs.at[0, h], loc.at[3]).start()
-    landed(qs.at[0], loc.at[2])
-    q_copy = remote(qs.at[0], qs.at[1], pair_s.at[0], pair_r.at[0], dev_pair)
-    q_copy.start()
-    landed(gs.at[0], loc.at[3])
-    g_copy = remote(gs.at[0], gs.at[1], pair_s.at[1], pair_r.at[1], dev_pair)
-    g_copy.start()
+    pairs = [(qs, remote(qs.at[0], qs.at[1], pair_s.at[0], pair_r.at[0], dev_pair))]
+    pairs.append((gs, remote(gs.at[0], gs.at[1], pair_s.at[1], pair_r.at[1], dev_pair)))
+    q_copy, g_copy = pairs[0][1], pairs[1][1]
+
+    def pair_send(w, gi):
+        landed(pairs[w][0].at[0], loc.at[2 + w])
+        pairs[w][1].start()
 
     def spans(cc):
         s0, s1 = span[2 * cc], span[2 * cc + 1]
@@ -222,8 +224,12 @@
     steps = {}
 
     def act(name, g=None):
-        for step, w, gi in POINTS[name] if g is None else POINTS[name].get(g, ()):
-            steps[step](w, gi)
+        for step, w, gi, *only in POINTS[name] if g is None else POINTS[name].get(g, ()):
+            todo = functools.partial(steps[step], w, gi)
+            if only:
+                pl.when(core == only[0])(todo)
+            else:
+                todo()
 
     def point(name, i):
         for g in POINTS[name]:
@@ -234,10 +240,11 @@
             pl.when(gi == g)(functools.partial(todo, g))
 
     steps["relay"], steps["send"] = y_relay, y_send
+    steps["zt"], steps["pair"] = zt_send, pair_send
+    act("early")
     y_send(0, 0)
+    act("first")
     prepare(0, qs, qn, qt)
-    steps["zt"] = zt_send
-    act("first")
     y_send(0, 1)
     y_send(0, 2)
     act("second")
@@ -518,10 +525,10 @@
             out[z, yy, w] = total.astype(BF16)
         ry_first(w, gi)
 
-    steps["merge"] = z_merge
+    steps["merge"], steps["open"] = z_merge, ry_first
 
     def value_step(i, carry):
-        gi = lax.rem(i + 1, NZ)
+        gi = NZ - 1 - i
         value_grads(gi)
         for g in range(1 if Z_FIRST else 0, NZ):
             pl.when(gi == g)(

time: 50.2 us -> 48.6 us (0.968)
  Pallas kernels: 49.3 us -> 47.8 us
    pallas_call x1, Pallas kernels: 48.6 us -> 47.1 us  [body(): pl.pallas_call(functools.partial(kernel, tps, heads), out_shape=tuple((pl...]
where the time goes in v4:
time: 48.6 us; the launch traced here: 48.4 us
  Pallas kernels  47.8 us (98%)
  between operations  0.64 us (1%)
    pallas_call x1, Pallas kernels, body(): pl.pallas_call(functools.partial(kernel, tps, heads), out_shape=tuple((pl...  47.1 us

profile of v4, /device:TPU:1, one launch (start us, length us, event | category | flops | bytes accessed | tf_op | source)
XLA Modules:
  0.0 48.4 jit_solution(18149779926601908380)
XLA Ops:
  0.6 47.1 %shard_map.76 = (bf16[128,1024]{1,0:T(8,128)(2,1)S(1)}, bf16[16,1024]{1,0:T(8,128)(2,1)S(1)}, bf16[16,1024]{1,0:T(8,128)(2,1)S(1)}) custom-call(s32[64]{0:T(128)} %span.1, bf16[128,1024]{1,0:T(8,128)(2,1)} %q_hbm.1, bf16[16,1024]{1,0:T(8,128)(2,1)} %k_hbm.1, bf16[16,1024]{1,0:T(8,128)(2,1)} %v_hbm.1, bf16[128,1024]{1,0:T(8,128)(2,1)} %g_hbm.1), custom_call_target="tpu_custom_call" | custom-call | tf_op jit(solution)/shard_map/pallas_call | solution.py:683
  47.7 0.7 %shard_map.77 = (bf16[128,1024]{1,0:T(8,128)(2,1)}, bf16[16,1024]{1,0:T(8,128)(2,1)}, bf16[16,1024]{1,0:T(8,128)(2,1)}) custom-call(bf16[128,1024]{1,0:T(8,128)(2,1)S(1)} %get-tuple-element.6.a, bf16[16,1024]{1,0:T(8,128)(2,1)S(1)} %get-tuple-element.7.b, bf16[16,1024]{1,0:T(8,128)(2,1)S(1)} %get-tuple-element.8.c), custom_call_target="tpu_custom_call" | custom-call | tf_op jit(solution)/shard_map/pallas_call | solution.py:694

commit v5 on v4

--- a/solution.py
+++ b/solution.py
@@ -19,9 +19,10 @@
 ZT_FIRST = ((0, 0), (0, 1), (0, 2), (0, 3))
 AG_RELAY = ()
 INNER_AHEAD = 1
+QUERY_CUT = 2
 Z_FIRST = ()
 RS_RELAY = ()
-POINTS = {'early': (('zt', 1, 0), ('zt', 1, 1, 0), ('zt', 1, 2, 0), ('zt', 1, 3, 0)), 'first': (('pair', 0, 0), ('send', 1, 0, 0)), 'second': (('pair', 1, 0),), 'third': (('zt', 1, 1, 1), ('zt', 1, 2, 1), ('zt', 1, 3, 1)), 'score': {0: (('send', 1, 1, 0), ('send', 1, 0, 1)), 1: (('send', 1, 2, 0),), 2: (('send', 1, 3, 0), ('send', 1, 1, 1)), 3: (('send', 1, 2, 1), ('send', 1, 3, 1))}, 'stats': (('inner', 1, 0),), 'value': {}, 'delta': (), 'key': {0: (('total', 1, 3),), 1: (('total', 1, 2),), 2: (('total', 1, 1),), 3: (('total', 1, 0),)}, 'keys': (), 'last': (('total', 0, 3), ('total', 0, 2)), 'end': (('total', 0, 1), ('total', 0, 0))}
+POINTS = {'early': (('zt', 1, 0), ('zt', 1, 1, 0), ('zt', 1, 2, 0), ('zt', 1, 3, 0)), 'first': (('pair', 0, 0), ('send', 1, 0, 0)), 'second': (('pair', 1, 0),), 'third': (('zt', 1, 1, 1), ('zt', 1, 2, 1), ('zt', 1, 3, 1)), 'score': {0: (('send', 1, 1, 0), ('send', 1, 0, 1)), 1: (('send', 1, 2, 0),), 2: (('send', 1, 3, 0), ('send', 1, 1, 1)), 3: (('send', 1, 2, 1), ('send', 1, 3, 1))}, 'stats': (('inner', 1, 0),), 'value': {}, 'delta': (), 'key': {0: (('total', 1, 3),), 1: (('total', 1, 2),), 2: (('total', 1, 1),), 3: (('total', 1, 0),)}, 'keys': (), 'last': (('total', 0, 2),), 'end': (('total', 0, 1), ('total', 0, 0)), 'middle': (('total', 0, 3),)}
 MESH = pl.DeviceIdType.MESH
 F32 = jnp.float32
 BF16 = jnp.bfloat16
@@ -34,7 +35,7 @@
 def kernel(
     tps,
     heads,
-    span,
+    span_hbm,
     q_hbm,
     k_hbm,
     v_hbm,
@@ -42,6 +43,7 @@
     dq_out,
     k_out,
     v_out,
+    span,
     kvst,
     kv,
     qs,
@@ -133,6 +135,8 @@
         ).start()
 
     fetch(0, k_hbm)
+    span_copy = pltpu.make_async_copy(span_hbm, span, loc.at[4])
+    span_copy.start()
 
     def z_of(gi):
         return lax.rem(z + gi + (gi // 2) * (1 - 2 * (gi % 2)), NZ)
@@ -173,6 +177,8 @@
     def pair_send(w, gi):
         landed(pairs[w][0].at[0], loc.at[2 + w])
         pairs[w][1].start()
+
+    span_copy.wait()
 
     def spans(cc):
         s0, s1 = span[2 * cc], span[2 * cc + 1]
@@ -569,11 +575,14 @@
     lax.fori_loop(0, NZ, key_step, 0)
 
     act("keys")
-    lax.fori_loop(0, NZ, query_step, 0)
+    lax.fori_loop(0, QUERY_CUT, query_step, 0)
+    act("middle")
+    lax.fori_loop(QUERY_CUT, NZ, query_step, 0)
     dqsend[...] = dqt[1].astype(BF16)
     dq_copy = remote(dqsend, dqrecv, pair_s.at[3], pair_r.at[3], dev_pair)
     dq_copy.start()
     act("last")
+    act("end")
     dq_copy.wait_recv()
     total_q = dqt[0] + dqrecv[...].astype(F32)
     lo, hi = total_q[0:HEAD, :].T.astype(BF16), total_q[HEAD : 2 * HEAD, :].T.astype(BF16)
@@ -581,7 +590,6 @@
     for h in range(heads):
         dq_out[0:SPAN, h * HEAD : (h + 1) * HEAD] = first[h * SPAN : (h + 1) * SPAN, :]
         dq_out[SPAN : 2 * SPAN, h * HEAD : (h + 1) * HEAD] = second[h * SPAN : (h + 1) * SPAN, :]
-    act("end")
     for w in range(2):
         kvr[z, w, t] = zs[0, w, own_rows]
 
@@ -629,6 +637,7 @@
     group = NY * SPAN
     dma = pltpu.SemaphoreType.DMA
     scratch = [
+        pltpu.SMEM(span_order.shape, jnp.int32),
         vmem((2, tps, tt, HEAD), BF16),
         vmem((NZ, NY, *block), BF16),
         vmem((2, heads, *half), BF16),
@@ -661,7 +670,7 @@
         vmem((NZ, *block), BF16),
         vmem((NZ, 2, tps, tt, HEAD), BF16),
         vmem((2, NY, *half), BF16),
-        dma((4,)),
+        dma((5,)),
         dma((2, NZ)),
         dma((2, NZ)),
         dma((2, NZ, 4)),
@@ -683,7 +692,7 @@
     grads = pl.pallas_call(
         functools.partial(kernel, tps, heads),
         out_shape=tuple(pltpu.VMEM(shape, BF16) for shape in shapes),
-        in_specs=[pl.BlockSpec(memory_space=pltpu.SMEM)] + [anywhere] * 4,
+        in_specs=[anywhere] * 5,
         out_specs=(in_vmem,) * 3,
         scratch_shapes=scratch,
         compiler_params=pltpu.CompilerParams(

time: 48.6 us -> 47.9 us (0.986)
  Pallas kernels: 47.8 us -> 47.1 us
    pallas_call x1, Pallas kernels: 47.1 us -> 46.4 us  [body(): pl.pallas_call(functools.partial(kernel, tps, heads), out_shape=tuple((pl...]
where the time goes in v5:
time: 47.9 us; the launch traced here: 47.7 us
  Pallas kernels  47.1 us (98%)
  between operations  0.64 us (1%)
    pallas_call x1, Pallas kernels, body(): pl.pallas_call(functools.partial(kernel, tps, heads), out_shape=tuple((pl...  46.4 us

profile of v5, /device:TPU:1, one launch (start us, length us, event | category | flops | bytes accessed | tf_op | source)
XLA Modules:
  0.0 47.7 jit_solution(15286503537097503837)
XLA Ops:
  0.6 46.4 %shard_map.76 = (bf16[128,1024]{1,0:T(8,128)(2,1)S(1)}, bf16[16,1024]{1,0:T(8,128)(2,1)S(1)}, bf16[16,1024]{1,0:T(8,128)(2,1)S(1)}) custom-call(s32[64]{0:T(128)} %span_hbm.1, bf16[128,1024]{1,0:T(8,128)(2,1)} %q_hbm.1, bf16[16,1024]{1,0:T(8,128)(2,1)} %k_hbm.1, bf16[16,1024]{1,0:T(8,128)(2,1)} %v_hbm.1, bf16[128,1024]{1,0:T(8,128)(2,1)} %g_hbm.1), custom_call_target="tpu_custom_call" | custom-call | tf_op jit(solution)/shard_map/pallas_call | solution.py:692
  47.0 0.7 %shard_map.77 = (bf16[128,1024]{1,0:T(8,128)(2,1)}, bf16[16,1024]{1,0:T(8,128)(2,1)}, bf16[16,1024]{1,0:T(8,128)(2,1)}) custom-call(bf16[128,1024]{1,0:T(8,128)(2,1)S(1)} %get-tuple-element.6.a, bf16[16,1024]{1,0:T(8,128)(2,1)S(1)} %get-tuple-element.7.b, bf16[16,1024]{1,0:T(8,128)(2,1)S(1)} %get-tuple-element.8.c), custom_call_target="tpu_custom_call" | custom-call | tf_op jit(solution)/shard_map/pallas_call | solution.py:703

commit v6 on v5

--- a/solution.py
+++ b/solution.py
@@ -150,7 +150,6 @@
             greet((ctx_of(z_of(gi), y, core), lax.rem(t + o, tps)))
     for device in (dev_yu, dev_yd, dev_yo, dev_pair):
         greet(device)
-    fetch(1, v_hbm)
     landed(kvst.at[0], loc.at[0])
     pl.semaphore_wait(barrier, NZ * tps - 1 + 4)
 
@@ -166,6 +165,7 @@
 
     for w, gi in ZT_FIRST:
         zt_send(w, gi)
+    fetch(1, v_hbm)
     for h in range(heads):
         cols = pl.ds(h * HEAD, HEAD)
         pltpu.make_async_copy(q_hbm.at[:, cols], qs.at[0, h], loc.at[2]).start()

time: 47.9 us -> 48 us (level)
  no operation moved by 1% of the time
where the time goes in v6:
time: 48 us; the launch traced here: 47.7 us
  Pallas kernels  47.1 us (98%)
  between operations  0.64 us (1%)
    pallas_call x1, Pallas kernels, body(): pl.pallas_call(functools.partial(kernel, tps, heads), out_shape=tuple((pl...  46.4 us

profile of v6, /device:TPU:1, one launch (start us, length us, event | category | flops | bytes accessed | tf_op | source)
XLA Modules:
  0.0 47.7 jit_solution(16354708342242155267)
XLA Ops:
  0.6 46.4 %shard_map.76 = (bf16[128,1024]{1,0:T(8,128)(2,1)S(1)}, bf16[16,1024]{1,0:T(8,128)(2,1)S(1)}, bf16[16,1024]{1,0:T(8,128)(2,1)S(1)}) custom-call(s32[64]{0:T(128)} %span_hbm.1, bf16[128,1024]{1,0:T(8,128)(2,1)} %q_hbm.1, bf16[16,1024]{1,0:T(8,128)(2,1)} %k_hbm.1, bf16[16,1024]{1,0:T(8,128)(2,1)} %v_hbm.1, bf16[128,1024]{1,0:T(8,128)(2,1)} %g_hbm.1), custom_call_target="tpu_custom_call" | custom-call | tf_op jit(solution)/shard_map/pallas_call | solution.py:692
  47.0 0.7 %shard_map.77 = (bf16[128,1024]{1,0:T(8,128)(2,1)}, bf16[16,1024]{1,0:T(8,128)(2,1)}, bf16[16,1024]{1,0:T(8,128)(2,1)}) custom-call(bf16[128,1024]{1,0:T(8,128)(2,1)S(1)} %get-tuple-element.6.a, bf16[16,1024]{1,0:T(8,128)(2,1)S(1)} %get-tuple-element.7.b, bf16[16,1024]{1,0:T(8,128)(2,1)S(1)} %get-tuple-element.8.c), custom_call_target="tpu_custom_call" | custom-call | tf_op jit(solution)/shard_map/pallas_call | solution.py:703
